TPU v7x, 32 devices: a whole 2x2x4 slice. The times are simulated.
32 devices in a mesh: dp: 8 (over y, x, core), tensor: 4 (over z).
Axes of the slice: x: 2, y: 2, z: 4, core: 2. Of those that a mesh axis runs over, the one named last changes fastest.
Arguments:
- tokens: bfloat16 [16384, 1024], P(('dp', 'tensor')), may hold values from -6 to 6
- lengths: int32 [8], P('dp'), may hold values from 120 to 2048, as said below
- ln1_gain: float32 [1024], replicated, may hold values from 0.1 to 1.9
- ln1_bias: float32 [1024], replicated, may hold values from -3 to 3
- w_query: bfloat16 [1024, 1024], P(None, 'tensor'), may hold values from -0.25 to 0.25
- w_key: bfloat16 [1024, 1024], P(None, 'tensor'), may hold values from -0.25 to 0.25
- w_value: bfloat16 [1024, 1024], P(None, 'tensor'), may hold values from -0.1875 to 0.1875
- w_out: bfloat16 [1024, 1024], P('tensor'), may hold values from -0.75 to 0.75
- ln2_gain: float32 [1024], replicated, may hold values from 0.1 to 1.9
- ln2_bias: float32 [1024], replicated, may hold values from -3 to 3
- w_gate: bfloat16 [1024, 4096], P(None, 'tensor'), may hold values from -0.1875 to 0.1875
- w_up: bfloat16 [1024, 4096], P(None, 'tensor'), may hold values from -0.1875 to 0.1875
- down_weight: bfloat16 [4096, 1024], P('tensor'), may hold values from -0.125 to 0.125
- cotangent: bfloat16 [16384, 1024], P(('dp', 'tensor')), may hold values from -6 to 6
Outputs:
- output: bfloat16 [16384, 1024], P(('dp', 'tensor'))
- input_grad: float32 [16384, 1024], P(('dp', 'tensor'))
- ln1_gain_grad: float32 [1024], replicated
- ln1_bias_grad: float32 [1024], replicated
- query_grad: float32 [1024, 1024], P(None, 'tensor')
- key_grad: float32 [1024, 1024], P(None, 'tensor')
- value_grad: float32 [1024, 1024], P(None, 'tensor')
- out_grad: float32 [1024, 1024], P('tensor')
- ln2_gain_grad: float32 [1024], replicated
- ln2_bias_grad: float32 [1024], replicated
- gate_grad: float32 [1024, 4096], P(None, 'tensor')
- up_grad: float32 [1024, 4096], P(None, 'tensor')
- down_grad: float32 [4096, 1024], P('tensor')
Inputs may be any that keep to these rules, and one draw needn't show every extreme that they name: `lengths`: real tokens of each window; every draw has a window of exactly 2048 and one of exactly 120.
All inputs are finite; a program needn't handle non-finite values.
Results may differ from a plain program's by a relative error of at most 0.023.
The roundings to bfloat16 on the way count: a program that leaves them out, or rounds other values in their place, can miss the bound.
Values may be sent and summed in bfloat16 or wider, within the bound.
A program may use at most 192 MiB of HBM per device.

v0:
```python
import functools
import math

import jax
import jax.numpy as jnp
from jax import lax
from jax.experimental import pallas as pl
from jax.experimental.pallas import tpu as pltpu
from jax.sharding import PartitionSpec as P

HD = 64
EPS = 1e-05
SCALE = 1.0 / math.sqrt(HD)
F32 = jnp.float32
BF = jnp.bfloat16
NT = (((1,), (1,)), ((), ()))
NN = (((1,), (0,)), ((), ()))
TN = (((0,), (0,)), ((), ()))
MESH = pl.DeviceIdType.MESH


def dot(a, b, dims=NN):
    return lax.dot_general(a, b, dims, preferred_element_type=F32)


def lanes(shape):
    return lax.broadcasted_iota(jnp.int32, shape, 1)


def split3(x):
    hi = x.astype(BF).astype(F32)
    mid = (x - hi).astype(BF).astype(F32)
    return hi, mid, x - hi - mid


def partner(x):
    width = x.shape[1]
    first = lanes(x.shape) % HD < HD // 2
    return jnp.where(first, pltpu.roll(x, width - HD // 2, 1), pltpu.roll(x, HD // 2, 1))


STEP = 64


def angle_tables(length):
    half = HD // 2
    lane = lax.optimization_barrier(lax.iota(jnp.int32, 2 * HD))
    freqs = 10000.0 ** (-((lane % half).astype(F32) * 2.0 / HD))
    sign = jnp.where(lane % HD < half, -1.0, 1.0)

    def table(positions):
        angles = positions[:, None] * freqs[None, :]
        return jnp.stack([jnp.cos(angles), jnp.sin(angles)])

    return table(lax.iota(F32, length // STEP) * STEP), table(lax.iota(F32, STEP)), sign[None, :]


def differ(a, b, bits):
    return sum(lax.rem(a // (1 << k) + b // (1 << k), 2) * (1 << k) for k in range(bits))


def remote(src, dst, send, recv, **to):
    return pltpu.make_async_remote_copy(
        src_ref=src, dst_ref=dst, send_sem=send, recv_sem=recv, device_id=to, device_id_type=MESH
    )


def ring(n, step):
    return lax.rem(lax.axis_index("tensor") + step, n)


def same_core(s, chips):
    me = lax.axis_index("dp")
    return differ(me // 2, s, chips.bit_length() - 1) * 2 + lax.rem(me, 2)


def sibling():
    me = lax.axis_index("dp")
    return me + 1 - 2 * lax.rem(me, 2)


def greet(n, chips, both_cores=False):
    barrier = pltpu.get_barrier_semaphore()
    if both_cores:
        pl.semaphore_signal(barrier, inc=1, device_id={"dp": sibling()}, device_id_type=MESH)
    for step in range(1, n):
        pl.semaphore_signal(barrier, inc=1, device_id={"tensor": ring(n, step)}, device_id_type=MESH)
    for s in range(1, chips):
        pl.semaphore_signal(
            barrier, inc=1, device_id={"dp": same_core(s, chips)}, device_id_type=MESH
        )
    pl.semaphore_wait(barrier, n + chips - 2 + both_cores)


def begin_kernel(
    n, chips, chunks, limit_ref, tokens_ref, ct_ref, gain_ref, shift_ref, wq_ref, wk_ref, wv_ref,
    coarse_ref, fine_ref, sign_ref, gate_ref, up_ref, down_ref,
    q_ref, k_ref, v_ref, cos_ref, sin_ref, rows_ref, gb_all, share_ref, landed, gb, columns, w_sem,
    right_send, right_recv, left_send, left_recv, gs_send, gs_recv, gr_send, gr_recv, keep_sem, rows_sem,
):
    me = lax.axis_index("tensor")
    place = lax.axis_index("dp")
    core = lax.rem(place, 2)
    bits = chips.bit_length() - 1
    rows, depth = tokens_ref.shape
    heads = q_ref.shape[0]
    piece = rows // chunks
    limit = limit_ref[0]

    def over(shard, d, c, send, recv, to):
        part = landed.at[shard, pl.ds(c * piece, piece)]
        return remote(part, part, send.at[d, c], recv.at[d, c], tensor=to)

    def rightward(d, c):
        return over(me - d, d, c, right_send, right_recv, me + 1)

    def leftward(d, c):
        return over(me + d, d, c, left_send, left_recv, me - 1)

    def from_left(d, c):
        return over(me - d, d - 1, c, right_send, right_recv, me - 1)

    def from_right(d, c):
        return over(me + d, d - 1, c, left_send, left_recv, me + 1)

    def spread_gb(c):
        return remote(
            gb, gb_all.at[place // 2, core], gs_send.at[c], gs_recv.at[c], dp=same_core(c, chips)
        )

    def relay_gb(c):
        there = gb_all.at[differ(place // 2, c, bits), core]
        return remote(there if c else gb, there, gr_send.at[c], gr_recv.at[c], dp=sibling())

    barrier = pltpu.get_barrier_semaphore()
    pl.semaphore_signal(barrier, inc=1, device_id={"dp": sibling()}, device_id_type=MESH)
    for s in range(1, chips):
        to = same_core(s, chips)
        pl.semaphore_signal(barrier, inc=1, device_id={"dp": to}, device_id_type=MESH)

    @pl.when(me > 0)
    def _():
        pl.semaphore_signal(barrier, inc=1, device_id={"tensor": me - 1}, device_id_type=MESH)

    @pl.when(me < n - 1)
    def _():
        pl.semaphore_signal(barrier, inc=1, device_id={"tensor": me + 1}, device_id_type=MESH)

    values = tokens_ref[...].astype(F32)
    values = values - jnp.mean(values, axis=1, keepdims=True)
    inverse = lax.rsqrt(jnp.mean(values * values, axis=1, keepdims=True) + EPS)
    landed[me] = (values * inverse * gain_ref[...] + shift_ref[...]).astype(BF)

    pl.semaphore_wait(barrier, chips + jnp.minimum(me, 1) + jnp.minimum(n - 1 - me, 1))

    for c in range(chunks):

        @pl.when(me < n - 1)
        def _():
            rightward(0, c).start()

        @pl.when(me > 0)
        def _():
            leftward(0, c).start()

    row = me * rows + lax.broadcasted_iota(jnp.int32, (rows, depth), 0)
    gb[...] = jnp.where(row < limit, ct_ref[...].astype(F32), 0.0).astype(BF)
    for s in range(1, chips):
        spread_gb(s).start()
    relay_gb(0).start()
    keep = pltpu.make_async_copy(gb, gb_all.at[place // 2, core], keep_sem)
    keep.start()
    share = share_ref.shape[1]
    aligned = share % 128 == 0
    ours = pl.ds(pl.multiple_of(place * share, share), share)
    cuts = [pltpu.make_async_copy(down_ref.at[ours], share_ref.at[2], w_sem.at[2])]
    for k, ref in enumerate((gate_ref, up_ref)):
        src = ref.at[:, ours] if aligned else ref
        cuts.append(pltpu.make_async_copy(src, columns.at[k], w_sem.at[k]))
    for cut in cuts:
        cut.start()

    lane = lanes((rows, 128))
    ones = jnp.where(lane < HD + 3, 1.0, 0.0)
    unit = jnp.where(lane == HD + 3, 1.0, 0.0)

    def put(out_ref, here, values, extra):
        for h in range(heads):
            own = values[:, h // 2 * 128 : h // 2 * 128 + 128]
            own = pltpu.roll(own, HD, 1) if h % 2 else own
            out_ref[h, here, :] = jnp.where(lane < HD, own, extra).astype(BF)

    def project(shard):
        here = pl.ds(pl.multiple_of(shard * rows, rows), rows)
        for i in range(rows // STEP):
            part = pl.ds(pl.multiple_of(shard * rows + i * STEP, STEP), STEP)
            coarse = pl.ds(shard * (rows // STEP) + i, 1)
            c0, s0 = coarse_ref[0, coarse, :], coarse_ref[1, coarse, :]
            cos_ref[part, :] = c0 * fine_ref[0] - s0 * fine_ref[1]
            sin_ref[part, :] = (s0 * fine_ref[0] + c0 * fine_ref[1]) * sign_ref[...]
        cosine = jnp.tile(cos_ref[here, :], (1, heads // 2))
        sine = jnp.tile(sin_ref[here, :], (1, heads // 2))
        x = landed[shard]
        row = shard * rows + lax.broadcasted_iota(jnp.int32, (rows, 128), 0)
        bias = jnp.where(lane == HD + 3, jnp.where(row < limit, 0.0, -1e30), ones)
        raw = dot(x, wq_ref[...])
        turned = (raw * cosine + partner(raw) * sine).astype(BF).astype(F32)
        put(q_ref, here, turned * SCALE, unit)
        raw = dot(x, wk_ref[...])
        put(k_ref, here, raw * cosine + partner(raw) * sine, bias)
        put(v_ref, here, dot(x, wv_ref[...]), ones)

    def save(shard):
        return pltpu.make_async_copy(landed.at[shard], rows_ref.at[shard], rows_sem.at[shard])

    for d in range(1, n + 1):
        for c in range(chunks):
            if d < n:

                @pl.when(me >= d)
                def _():
                    from_left(d, c).wait_recv()

                @pl.when((me >= d) & (me < n - 1))
                def _():
                    rightward(d, c).start()

                @pl.when(me + d < n)
                def _():
                    from_right(d, c).wait_recv()

                @pl.when((me + d < n) & (me > 0))
                def _():
                    leftward(d, c).start()

            if c == 0:

                @pl.when(me >= d - 1)
                def _():
                    save(me - d + 1).start()
                    project(me - d + 1)

            if c == 2 and d == 1:
                for cut in cuts:
                    cut.wait()
                for k in range(2):
                    share_ref[k] = columns[k].astype(F32).T.astype(BF)

            if c == 1 and d > 1:

                @pl.when(me + d - 1 < n)
                def _():
                    save(me + d - 1).start()
                    project(me + d - 1)

            if c == chunks - 1 and d == 2:
                for s in range(1, chips // 2 + 1):
                    spread_gb(s).wait_recv()
                    relay_gb(s).start()

            if c == 0 and d == n:
                for s in range(chips // 2 + 1, chips):
                    spread_gb(s).wait_recv()
                    relay_gb(s).start()

    for d in range(n - 1):
        for c in range(chunks):

            @pl.when((me >= d) & (me < n - 1))
            def _():
                rightward(d, c).wait_send()

            @pl.when((me + d < n) & (me > 0))
            def _():
                leftward(d, c).wait_send()

    for s in range(chips):
        relay_gb(s).wait()
        if s:
            spread_gb(s).wait_send()
    keep.wait()
    for shard in range(n):
        save(shard).wait()


def begin(
    tokens, cotangent, gain, shift, w_query, w_key, w_value, tables, gate, up, down, limit, n, devices
):
    rows, depth = tokens.shape
    total = n * rows
    heads = w_query.shape[1] // HD
    chips = devices // 2
    chunks = 4
    share = down.shape[0] // devices
    if share % 128:
        place = lax.axis_index("dp")
        gate, up = (lax.dynamic_slice_in_dim(w, place * share, share, 1) for w in (gate, up))
    vmem = pl.BlockSpec(memory_space=pltpu.VMEM)
    hbm = pl.BlockSpec(memory_space=pl.ANY)
    return pl.pallas_call(
        functools.partial(begin_kernel, n, chips, chunks),
        out_shape=(jax.ShapeDtypeStruct((heads, total, 128), BF),) * 3
        + (jax.ShapeDtypeStruct((total, 128), F32),) * 2
        + (
            jax.ShapeDtypeStruct((n, rows, depth), BF),
            jax.ShapeDtypeStruct((chips, 2, rows, depth), BF),
            jax.ShapeDtypeStruct((3, share, depth), BF),
        ),
        in_specs=[pl.BlockSpec(memory_space=pltpu.SMEM)] + [vmem] * 10 + [hbm] * 3,
        out_specs=[vmem] * 5 + [hbm] * 2 + [vmem],
        scratch_shapes=[pltpu.VMEM((n, rows, depth), BF), pltpu.VMEM((rows, depth), BF)]
        + [pltpu.VMEM((2, depth, share), BF), pltpu.SemaphoreType.DMA((3,))]
        + [pltpu.SemaphoreType.DMA((n - 1, chunks))] * 4
        + [pltpu.SemaphoreType.DMA((chips,))] * 4
        + [pltpu.SemaphoreType.DMA, pltpu.SemaphoreType.DMA((n,))],
        compiler_params=pltpu.CompilerParams(
            vmem_limit_bytes=44 << 20, collective_id=5, has_side_effects=True
        ),
        cost_estimate=pl.CostEstimate(
            flops=6 * total * depth * heads * HD * 10, bytes_accessed=30 << 20, transcendentals=0
        ),
        name="begin",
    )(
        limit, tokens, cotangent, gain.reshape(1, depth), shift.reshape(1, depth),
        w_query, w_key, w_value, *tables, gate, up, down,
    )


def att_fwd_kernel(
    n, chips, q_ref, k_ref, v_ref, wo_ref,
    ctx_ref, lse_ref, out_ref, wo_z, wo_all, send_sem, recv_sem, own_sem,
    wz_send, wz_recv, ws_send, ws_recv, wr_send, wr_recv, keep_sem,
):
    s = pl.program_id(0)
    h = pl.program_id(1)
    heads = pl.num_programs(1)
    rows = q_ref.shape[1] // n
    me = lax.axis_index("tensor")
    place = lax.axis_index("dp")
    core = lax.rem(place, 2)
    bits = chips.bit_length() - 1

    def wo_over(step):
        return remote(
            wo_ref, wo_z.at[me], wz_send.at[step], wz_recv.at[step], tensor=ring(n, step + 1)
        )

    def spread_wo(c):
        return remote(
            wo_z, wo_all.at[:, place], ws_send.at[c], ws_recv.at[c], dp=same_core(c, chips)
        )

    def relay_wo(c):
        there = wo_all.at[:, differ(place // 2, c, bits) * 2 + core]
        return remote(there if c else wo_z, there, wr_send.at[c], wr_recv.at[c], dp=sibling())

    keeps = [
        pltpu.make_async_copy(wo_ref, wo_z.at[me], keep_sem.at[0]),
        pltpu.make_async_copy(wo_z, wo_all.at[:, place], keep_sem.at[1]),
    ]

    @pl.when((s == 0) & (h == 0))
    def _():
        greet(n, chips, True)
        for step in range(n - 1):
            wo_over(step).start()
        keeps[0].start()

    @pl.when((s == 1) & (h == 0))
    def _():
        for step in range(n - 1):
            wo_over(step).wait()
        keeps[0].wait()
        for c in range(1, chips):
            spread_wo(c).start()
        relay_wo(0).start()
        keeps[1].start()

    @pl.when((s == n - 1) & (h == 0))
    def _():
        for c in range(1, chips):
            spread_wo(c).wait_recv()
            relay_wo(c).start()

    owner = ring(n, s + 1)
    block = pl.ds(pl.multiple_of(owner * rows, rows), rows)
    scores = dot(q_ref[h, block, :], k_ref[h], NT)
    peak = jnp.max(scores, axis=1, keepdims=True)
    acc = dot(jnp.exp(scores - peak).astype(BF), v_ref[h])
    lane = lanes((rows, 128))
    total = jnp.sum(jnp.where(lane == HD, acc, 0.0), axis=1, keepdims=True)
    out = acc * (1.0 / total)
    odd = lax.rem(h, 2)
    out = jnp.where(odd == 1, pltpu.roll(out, HD, 1), out).astype(BF)
    pair = pl.ds(pl.multiple_of(h // 2 * 128, 128), 128)
    ctx_ref[block, pair] = jnp.where((lane >= HD) == (odd == 1), out, ctx_ref[block, pair])
    lse_ref[block, :] = jnp.where(lane == h, peak + jnp.log(total), lse_ref[block, :])

    def push(step):
        return pltpu.make_async_remote_copy(
            src_ref=ctx_ref.at[block],
            dst_ref=out_ref.at[me],
            send_sem=send_sem.at[step],
            recv_sem=recv_sem.at[step],
            device_id={"tensor": owner},
            device_id_type=MESH,
        )

    @pl.when((h == heads - 1) & (s < n - 1))
    def _():
        push(s).start()

    @pl.when((h == heads - 1) & (s == n - 1))
    def _():
        keep = pltpu.make_async_copy(ctx_ref.at[block], out_ref.at[me], own_sem)
        keep.start()
        for step in range(n - 1):
            push(step).wait()
        keep.wait()
        keeps[1].wait()
        for c in range(chips):
            relay_wo(c).wait()
            if c:
                spread_wo(c).wait_send()


def att_fwd(q, k, v, w_out_piece, n, devices):
    heads, total, _ = q.shape
    width = heads * HD
    rows = total // n
    share, depth = w_out_piece.shape
    chips = devices // 2
    hbm = pl.BlockSpec(memory_space=pl.ANY)

    def whole(*shape):
        return pl.BlockSpec(shape, lambda *_: (0,) * len(shape), pipeline_mode=pl.Buffered(1))

    return pl.pallas_call(
        functools.partial(att_fwd_kernel, n, chips),
        out_shape=(
            jax.ShapeDtypeStruct((total, width), BF),
            jax.ShapeDtypeStruct((total, 128), F32),
            jax.ShapeDtypeStruct((n, rows, width), BF),
            jax.ShapeDtypeStruct((n, share, depth), BF),
            jax.ShapeDtypeStruct((n, devices, share, depth), BF),
        ),
        grid_spec=pltpu.PrefetchScalarGridSpec(
            num_scalar_prefetch=0,
            grid=(n, heads),
            in_specs=[whole(heads, total, 128)] * 3 + [hbm],
            out_specs=[whole(total, width), whole(total, 128)] + [hbm] * 3,
            scratch_shapes=[pltpu.SemaphoreType.DMA((n - 1,))] * 2
            + [pltpu.SemaphoreType.DMA]
            + [pltpu.SemaphoreType.DMA((n - 1,))] * 2
            + [pltpu.SemaphoreType.DMA((chips,))] * 4
            + [pltpu.SemaphoreType.DMA((2,))],
        ),
        compiler_params=pltpu.CompilerParams(
            vmem_limit_bytes=40 << 20, collective_id=1, has_side_effects=True
        ),
        cost_estimate=pl.CostEstimate(
            flops=4 * total * total * 256 * heads,
            bytes_accessed=10 * total * width,
            transcendentals=total * total * heads,
        ),
        name="att_fwd",
    )(q, k, v, w_out_piece)


def att_bwd_kernel(
    n, bk, chips, ga_ref, wo_ref, cown_ref, parts_ref, q_ref, k_ref, v_ref, ctx_ref, lse_ref,
    cos_ref, sin_ref, pk_ref, own_ref, sums_ref, og_ref, do, gc, dka, dva, dqs,
    og_full, og_own, og_mate, og_sib, og_land, og_piece, og_z,
    send_sem, recv_sem, out_send, out_recv, pk_send, pk_recv, keep_sem,
    om_send, om_recv, op_send, op_recv, oz_send, oz_recv,
):
    i = pl.program_id(0)
    heads, total, _ = k_ref.shape
    h = jnp.where(i < heads, i, (i - heads) // (n - 1))
    t = jnp.where(i < heads, 0, lax.rem(i - heads, n - 1) + 1)
    rows = total // n
    me = lax.axis_index("tensor")
    place = lax.axis_index("dp")
    core = lax.rem(place, 2)
    bits = chips.bit_length() - 1
    share = og_ref.shape[0]
    mine = pl.ds(pl.multiple_of(me * rows, rows), rows)

    def push(step):
        return remote(
            gc.at[step], do.at[mine], send_sem.at[step], recv_sem.at[step], tensor=ring(n, step + 1)
        )

    def push_out(s):
        return remote(
            parts_ref.at[s], sums_ref.at[s - 1], out_send.at[s - 1], out_recv.at[s - 1],
            dp=same_core(s, chips),
        )

    def columns(slot):
        return pl.ds(pl.multiple_of(slot * 128, 128), 128)

    def push_pack(slot, step):
        owner = ring(n, step + 1)
        return remote(
            pk_ref.at[pl.ds(pl.multiple_of(owner * rows, rows), rows), columns(slot)],
            own_ref.at[me, :, columns(slot)],
            pk_send.at[slot, step], pk_recv.at[slot, step], tensor=owner,
        )

    def keep(slot):
        return pltpu.make_async_copy(
            pk_ref.at[mine, columns(slot)], own_ref.at[me, :, columns(slot)], keep_sem.at[slot]
        )

    @pl.when(i == 0)
    def _():
        greet(n, chips, True)

        def send(step, carry):
            gc[step] = dot(ga_ref[...], wo_ref[ring(n, step + 1)], NT).astype(BF)
            push(step).start()
            return carry

        lax.fori_loop(0, n - 1, send, 0)
        do[mine, :] = dot(ga_ref[...], wo_ref[me], NT).astype(BF)

    def og_swap():
        return remote(og_mate, og_sib, om_send, om_recv, dp=sibling())

    def og_push(s):
        return remote(og_sib.at[s], og_land.at[s], op_send.at[s], op_recv.at[s], dp=same_core(s, chips))

    def og_over(step):
        to = ring(n, step + 1)
        return remote(og_piece.at[to], og_z.at[me], oz_send.at[step], oz_recv.at[step], tensor=to)

    @pl.when(i == 1)
    def _():
        def term(part, carry):
            og_full[...] = dot(cown_ref[part], ga_ref[...], TN)
            for s in range(chips):
                start = differ(place // 2, s, bits) * 2
                here = pl.ds(pl.multiple_of((start + core) * share, share), share)
                there = pl.ds(pl.multiple_of((start + 1 - core) * share, share), share)
                og_own[s, part] = og_full[here, :]
                og_mate[s, part] = og_full[there, :].astype(BF)
            return carry

        lax.fori_loop(0, n, term, 0)
        og_swap().start()

    @pl.when(i == 2)
    def _():
        og_swap().wait_recv()
        for s in range(chips):
            og_sib[s] = (og_own[s] + og_sib[s].astype(F32)).astype(BF)
            if s:
                og_push(s).start()

    @pl.when(i == heads + 2)
    def _():
        joined = og_sib[0].astype(F32)
        for s in range(1, chips):
            og_push(s).wait_recv()
            joined = joined + og_land[s].astype(F32)
        og_piece[...] = joined.astype(BF)
        for step in range(n - 1):
            og_over(step).start()
        for s in range(1, chips):
            push_out(s).start()

    @pl.when(i == heads * n - 1)
    def _():
        og_z[me] = og_piece[me]
        for step in range(n - 1):
            og_over(step).wait_recv()
        joined = og_z[0].astype(F32)
        for part in range(1, n):
            joined = joined + og_z[part].astype(F32)
        og_ref[...] = joined.astype(BF)

    @pl.when((h == 0) & (t > 0))
    def _():
        push(t - 1).wait_recv()

    source = ring(n, n - t)
    block = pl.ds(pl.multiple_of(source * rows, rows), rows)
    pair = columns(h // 2)
    odd = lax.rem(h, 2) == 1
    lane = lanes((rows, 128))
    off = lane - HD
    logsum = jnp.sum(jnp.where(lane == h, lse_ref[block, :], 0.0), axis=1, keepdims=True)
    a, b, c = split3(-logsum)
    q = q_ref[h, block, :].astype(F32)
    q = jnp.where(off == 0, a, jnp.where(off == 1, b, jnp.where(off == 2, c, q))).astype(BF)
    g = jnp.where((lane >= HD) == odd, do[block, pair].astype(F32), 0.0)
    delta = jnp.sum(g * ctx_ref[block, pair].astype(F32), axis=1, keepdims=True)
    a, b, c = split3(-delta)
    g = jnp.where(odd, pltpu.roll(g, HD, 1), g)
    g = jnp.where(off == 0, a, jnp.where(off == 1, b, jnp.where(off == 2, c, g))).astype(BF)
    acc = jnp.zeros((rows, 128), F32)
    for j in range(total // bk):
        rk = pl.ds(j * bk, bk)
        kt = k_ref[h, rk, :]
        probs = jnp.exp(dot(kt, q, NT))
        grad = (probs * dot(v_ref[h, rk, :], g, NT)).astype(BF)
        for sums, term in ((dva, dot(probs.astype(BF), g)), (dka, dot(grad, q))):
            before = jnp.where(t == 0, jnp.zeros_like(term), sums[h, rk, :])
            sums[h, rk, :] = before + term
        acc = acc + dot(grad, kt, TN)
    acc = acc * SCALE

    @pl.when(jnp.logical_not(odd))
    def _():
        dqs[block, :] = acc

    @pl.when(odd)
    def _():
        grad = jnp.where(lane < HD, dqs[block, :], pltpu.roll(acc, HD, 1))
        grad = grad * cos_ref[block, :] - partner(grad) * sin_ref[block, :]
        pk_ref[block, columns(heads + h // 2)] = grad.astype(BF)

    @pl.when(odd & (t == 0))
    def _():
        keep(heads + h // 2).start()

    @pl.when(odd & (t > 0))
    def _():
        push_pack(heads + h // 2, n - 1 - t).start()

    @pl.when(t == n - 1)
    def _():
        dk = dka[h]
        dk = dk * cos_ref[...] - partner(dk) * sin_ref[...]
        both = jnp.where(lanes((total, 128)) < HD, dk, pltpu.roll(dva[h], HD, 1))
        pk_ref[:, columns(h)] = both.astype(BF)
        for step in range(n - 1):
            push_pack(h, step).start()
        keep(h).start()

    @pl.when(i == heads * n - 1)
    def _():
        for step in range(n - 1):
            push(step).wait_send()
        for s in range(1, chips):
            push_out(s).wait()
        og_swap().wait_send()
        for s in range(1, chips):
            og_push(s).wait_send()
        for step in range(n - 1):
            og_over(step).wait_send()
        for slot in range(heads + heads // 2):
            keep(slot).wait()
            for step in range(n - 1):
                push_pack(slot, step).wait()


def att_bwd(grad_attn, w_out, ctx_own, parts, q, k, v, ctx, lse, cosine, sine, n, bk=512):
    heads, total, _ = q.shape
    width = heads * HD
    rows, depth = grad_attn.shape
    chips = parts.shape[0]
    share = width // (2 * chips)
    slots = heads + heads // 2
    hbm = pl.BlockSpec(memory_space=pl.ANY)

    def whole(*shape):
        return pl.BlockSpec(shape, lambda *_: (0,) * len(shape), pipeline_mode=pl.Buffered(1))

    return pl.pallas_call(
        functools.partial(att_bwd_kernel, n, bk, chips),
        out_shape=(
            jax.ShapeDtypeStruct((total, slots * 128), BF),
            jax.ShapeDtypeStruct((n, rows, slots * 128), BF),
            jax.ShapeDtypeStruct((chips - 1, rows, depth), BF),
            jax.ShapeDtypeStruct((share, depth), BF),
        ),
        grid_spec=pltpu.PrefetchScalarGridSpec(
            num_scalar_prefetch=0,
            grid=(heads * n,),
            in_specs=[whole(rows, depth), whole(n, width, depth), whole(n, rows, width), hbm]
            + [whole(heads, total, 128)] * 3
            + [whole(total, width)]
            + [whole(total, 128)] * 3,
            out_specs=[whole(total, slots * 128), hbm, hbm, whole(share, depth)],
            scratch_shapes=[
                pltpu.VMEM((total, width), BF),
                pltpu.VMEM((n - 1, rows, width), BF),
            ]
            + [pltpu.VMEM((heads, total, 128), F32)] * 2
            + [pltpu.VMEM((total, 128), F32)]
            + [
                pltpu.VMEM((width, depth), F32),
                pltpu.VMEM((chips, n, share, depth), F32),
                pltpu.VMEM((chips, n, share, depth), BF),
                pltpu.VMEM((chips, n, share, depth), BF),
                pltpu.VMEM((chips, n, share, depth), BF),
                pltpu.VMEM((n, share, depth), BF),
                pltpu.VMEM((n, share, depth), BF),
            ]
            + [pltpu.SemaphoreType.DMA((n - 1,))] * 2
            + [pltpu.SemaphoreType.DMA((chips - 1,))] * 2
            + [pltpu.SemaphoreType.DMA((slots, n - 1))] * 2
            + [pltpu.SemaphoreType.DMA((slots,))]
            + [pltpu.SemaphoreType.DMA] * 2
            + [pltpu.SemaphoreType.DMA((chips,))] * 2
            + [pltpu.SemaphoreType.DMA((n - 1,))] * 2,
        ),
        compiler_params=pltpu.CompilerParams(
            vmem_limit_bytes=56 << 20, collective_id=2, has_side_effects=True
        ),
        cost_estimate=pl.CostEstimate(
            flops=10 * total * total * 256 * heads,
            bytes_accessed=20 * total * width,
            transcendentals=total * total * heads,
        ),
        name="att_bwd",
    )(grad_attn, w_out, ctx_own, parts, q, k, v, ctx, lse, cosine, sine)


def finish_kernel(
    chips, n, width, x_ref, pk_ref, own_ref, w_ref, tokens_ref, middle_ref, gain_ref, vec_ref,
    input_ref, q_ref, k_ref, v_ref, sums_ref,
    full, mate, sib, land, fin, every, vec_z, vec_dp, vec_me,
    sx_send, sx_recv, rs_send, rs_recv, ag_send, ag_recv, rl_send, rl_recv,
    vz_send, vz_recv, vd_send, vd_recv, own_sem,
):
    bits = chips.bit_length() - 1
    me = lax.axis_index("dp")
    place = lax.axis_index("tensor")
    core = lax.rem(me, 2)
    chip = me // 2
    other = 1 - core
    heads = width // HD
    piece = fin.shape[0]

    def swap(s):
        return remote(mate.at[s], sib.at[s], sx_send.at[s], sx_recv.at[s], dp=chip * 2 + other)

    def push(s):
        return remote(sib.at[s], land.at[s], rs_send.at[s], rs_recv.at[s], dp=same_core(s, chips))

    def spread(s):
        return remote(
            fin, every.at[chip, core], ag_send.at[s], ag_recv.at[s], dp=same_core(s, chips)
        )

    def relay(s):
        src = every.at[differ(chip, s, bits), core]
        return remote(src, src, rl_send.at[s], rl_recv.at[s], dp=chip * 2 + other)

    def vec_over(step):
        return remote(
            vec_me.at[0], vec_z.at[place], vz_send.at[step], vz_recv.at[step], tensor=ring(n, step + 1)
        )

    def vec_across(step):
        return remote(
            vec_me.at[1], vec_dp.at[me], vd_send.at[step], vd_recv.at[step],
            dp=lax.rem(me + step + 1, 2 * chips),
        )

    barrier = pltpu.get_barrier_semaphore()
    for step in range(n - 1):
        pl.semaphore_signal(barrier, inc=1, device_id={"tensor": ring(n, step + 1)}, device_id_type=MESH)
    for step in range(2 * chips - 1):
        to = lax.rem(me + step + 1, 2 * chips)
        pl.semaphore_signal(barrier, inc=1, device_id={"dp": to}, device_id_type=MESH)

    full[...] = dot(x_ref[...], pk_ref[...], TN)
    pl.semaphore_wait(barrier, n + 2 * chips - 2)

    def part(s, which):
        start = (differ(chip, s, bits) * 2 + which) * piece
        return full[pl.ds(pl.multiple_of(start, piece), piece), :]

    for s in range(chips):
        mate[s] = part(s, other).astype(BF)
        swap(s).start()

    grad = jnp.zeros(input_ref.shape, F32)
    for t in range(n):
        w = w_ref[:, t].reshape(w_ref.shape[0] * w_ref.shape[2], w_ref.shape[3])
        grad = grad + dot(own_ref[t], w, NT).astype(BF).astype(F32)

    for s in range(1, chips):
        swap(s).wait_recv()
        sib[s] = (sib[s].astype(F32) + part(s, core)).astype(BF)
        push(s).start()
    swap(0).wait_recv()
    total = sib[0].astype(F32) + part(0, core)

    values = tokens_ref[...].astype(F32)
    values = values - jnp.mean(values, axis=1, keepdims=True)
    inverse = lax.rsqrt(jnp.mean(values * values, axis=1, keepdims=True) + EPS)
    scaled = values * inverse
    through = grad * gain_ref[...]
    inner = through - jnp.mean(through, axis=1, keepdims=True)
    inner = inner - scaled * jnp.mean(through * scaled, axis=1, keepdims=True)
    input_ref[...] = middle_ref[...] + inverse * inner
    vec_me[0, 0:1] = jnp.sum(grad * scaled, axis=0, keepdims=True)
    vec_me[0, 1:2] = jnp.sum(grad, axis=0, keepdims=True)
    vec_me[0, 2:4] = vec_ref[...]
    vec_me[0, 4:8] = jnp.zeros((4, vec_ref.shape[1]), F32)
    vec_z[place] = vec_me[0]
    for step in range(n - 1):
        vec_over(step).start()

    for s in range(1, chips):
        push(s).wait_recv()
        total = total + land[s].astype(F32)
    fin[...] = total.astype(BF)
    for s in range(1, chips):
        spread(s).start()
    mine = pltpu.make_async_copy(fin, every.at[chip, core], own_sem)
    mine.start()
    mine.wait()
    relay(0).start()

    for step in range(n - 1):
        vec_over(step).wait()
    vec = vec_z[0]
    for t in range(1, n):
        vec = vec + vec_z[t]
    vec_me[1] = vec
    vec_dp[me] = vec
    for step in range(2 * chips - 1):
        vec_across(step).start()
    for s in range(1, chips):
        spread(s).wait_recv()
        relay(s).start()
    for step in range(2 * chips - 1):
        vec_across(step).wait()
    vec = vec_dp[0]
    for t in range(1, 2 * chips):
        vec = vec + vec_dp[t]
    sums_ref[...] = vec
    for s in range(chips):
        relay(s).wait()
        swap(s).wait_send()
        if s > 0:
            spread(s).wait_send()
            push(s).wait_send()
    first = lanes((piece, 128)) < HD
    for d in range(2 * chips):
        rows = slice(d * piece, (d + 1) * piece)
        g = every[d // 2, d % 2].astype(F32)
        for pair in range(heads // 2):
            a = g[:, pair * 256 : pair * 256 + 128]
            b = g[:, pair * 256 + 128 : pair * 256 + 256]
            out = slice(pair * 128, pair * 128 + 128)
            q_ref[rows, out] = g[:, (heads + pair) * 128 : (heads + pair + 1) * 128]
            k_ref[rows, out] = jnp.where(first, a, pltpu.roll(b, HD, 1))
            v_ref[rows, out] = jnp.where(first, pltpu.roll(a, HD, 1), b)


def finish(rows_all, packed, own, w_all, tokens, middle, gain, vec, width, devices):
    n, rows, packs = own.shape
    depth = tokens.shape[1]
    chips = devices // 2
    piece = depth // devices
    vmem = pl.BlockSpec(memory_space=pltpu.VMEM)
    out = jax.ShapeDtypeStruct((depth, width), F32)
    return pl.pallas_call(
        functools.partial(finish_kernel, chips, n, width),
        out_shape=(
            jax.ShapeDtypeStruct((rows, depth), F32), out, out, out,
            jax.ShapeDtypeStruct((8, depth), F32),
        ),
        in_specs=[vmem] * 8,
        out_specs=[vmem] * 5,
        scratch_shapes=[
            pltpu.VMEM((depth, packs), F32),
            pltpu.VMEM((chips, piece, packs), BF),
            pltpu.VMEM((chips, piece, packs), BF),
            pltpu.VMEM((chips, piece, packs), BF),
            pltpu.VMEM((piece, packs), BF),
            pltpu.VMEM((chips, 2, piece, packs), BF),
            pltpu.VMEM((n, 8, depth), F32),
            pltpu.VMEM((devices, 8, depth), F32),
            pltpu.VMEM((2, 8, depth), F32),
        ]
        + [pltpu.SemaphoreType.DMA((chips,))] * 8
        + [pltpu.SemaphoreType.DMA((n - 1,))] * 2
        + [pltpu.SemaphoreType.DMA((devices - 1,))] * 2
        + [pltpu.SemaphoreType.DMA],
        compiler_params=pltpu.CompilerParams(
            vmem_limit_bytes=56 << 20, collective_id=4, has_side_effects=True
        ),
        cost_estimate=pl.CostEstimate(
            flops=4 * n * rows * depth * packs, bytes_accessed=20 << 20, transcendentals=0
        ),
        name="finish",
    )(rows_all, packed, own, w_all, tokens, middle, gain.reshape(1, depth), vec)


def ffn_kernel(
    chips, x_ref, gb_ref, w_ref, wp_ref, dx_ref, out_ref, dw_ref, wp_z,
    rows_all, gb, hid, gate_g, up_g, own, sib, mate,
    ag_send, ag_recv, rl_send, rl_recv, sx_send, sx_recv, rs_send, rs_recv, fw_send, fw_recv,
    gb_sem, out_sem, dx_sem, wp_send, wp_recv, wp_sem,
):
    bits = chips.bit_length() - 1
    me = lax.axis_index("dp")
    core = lax.rem(me, 2)
    chip = me // 2
    other = 1 - core
    rows, depth = x_ref.shape
    n = dw_ref.shape[0]
    share = dw_ref.shape[2]

    def spread(s):
        to = differ(chip, s, bits) * 2 + core
        return remote(x_ref, rows_all.at[chip, core], ag_send.at[s], ag_recv.at[s], dp=to)

    square = chips == 4

    def hand_on(s):
        half = pl.ds((s - 1) * (rows // 2), rows // 2)
        part = rows_all.at[differ(chip, s, bits), core, half]
        to = differ(chip, 3 - s, bits) * 2 + core
        return remote(part, part, fw_send.at[s], fw_recv.at[s], dp=to)

    def handed(s):
        half = pl.ds((s - 1) * (rows // 2), rows // 2)
        part = rows_all.at[differ(chip, 3, bits), core, half]
        to = differ(chip, 3 - s, bits) * 2 + core
        return remote(part, part, fw_send.at[s], fw_recv.at[s], dp=to)

    def relay(s):
        src = differ(chip, s, bits)
        return remote(
            rows_all.at[src, core], rows_all.at[src, core], rl_send.at[s], rl_recv.at[s],
            dp=chip * 2 + other,
        )

    def swap(s):
        return remote(
            mate.at[lax.rem(s, 2)], sib.at[s], sx_send.at[s], sx_recv.at[s], dp=chip * 2 + other
        )

    def push(s):
        to = differ(chip, s, bits) * 2 + core
        return remote(sib.at[s, 0], dx_ref.at[s], rs_send.at[s], rs_recv.at[s], dp=to)

    def fetch(s):
        src = differ(chip, s, bits)
        return pltpu.make_async_copy(gb_ref.at[src], gb.at[src], gb_sem.at[s])

    part = lax.axis_index("tensor")

    def over(step):
        return remote(
            wp_ref, wp_z.at[part], wp_send.at[step], wp_recv.at[step], tensor=ring(n, step + 1)
        )

    def keep(s):
        return pltpu.make_async_copy(sib.at[s, 1], out_ref.at[s], out_sem.at[s])

    for s in range(chips):
        fetch(s).start()
    barrier = pltpu.get_barrier_semaphore()
    for step in range(1, n):
        pl.semaphore_signal(barrier, inc=1, device_id={"tensor": ring(n, step)}, device_id_type=MESH)
    pl.semaphore_signal(barrier, inc=1, device_id={"dp": chip * 2 + other}, device_id_type=MESH)
    for s in range(1, chips):
        to = differ(chip, s, bits) * 2 + core
        pl.semaphore_signal(barrier, inc=1, device_id={"dp": to}, device_id_type=MESH)
    pl.semaphore_wait(barrier, chips + n - 1)
    direct = range(1, 3) if square else range(1, chips)
    for s in direct:
        spread(s).start()
    mine = pltpu.make_async_copy(x_ref, rows_all.at[chip, core], ag_send.at[0])
    mine.start()
    mine.wait()
    relay(0).start()
    for step in range(n - 1):
        over(step).start()
    keep_wp = pltpu.make_async_copy(wp_ref, wp_z.at[part], wp_sem)
    keep_wp.start()

    def shard(src, which, put):
        x = rows_all[src, which]
        grad = gb[src, which]
        gate = dot(x, w_ref[0], NT)
        upper = dot(x, w_ref[1], NT)
        grad_hidden = dot(grad, w_ref[2], NT)
        sigma = jax.nn.sigmoid(gate)
        act = gate * sigma
        hidden = (act * upper).astype(BF)
        grad_gate = (grad_hidden * upper * sigma * (1.0 + gate * (1.0 - sigma))).astype(BF)
        grad_upper = (grad_hidden * act).astype(BF)
        hid[src, which] = hidden
        gate_g[src, which] = grad_gate
        up_g[src, which] = grad_upper
        put[0] = (dot(grad_gate, w_ref[0]) + dot(grad_upper, w_ref[1])).astype(BF)
        put[1] = dot(hidden, w_ref[2]).astype(BF)

    def step(s, carry):
        src = differ(chip, s, bits)
        slot = lax.rem(s, 2)
        relay(s).wait_recv()
        fetch(s).wait()

        @pl.when(s >= 2)
        def _():
            swap(s - 2).wait_send()

        shard(src, other, mate.at[slot])
        swap(s).start()
        shard(src, core, own)
        swap(s).wait_recv()
        for k in range(2):
            sib[s, k] = (sib[s, k].astype(F32) + own[k].astype(F32)).astype(BF)

        @pl.when(s > 0)
        def _():
            push(s).start()

        keep(s).start()

        if square:

            @pl.when(s == 0)
            def _():
                for near in (1, 2):
                    spread(near).wait_recv()
                    hand_on(near).start()
                    relay(near).start()

        else:

            @pl.when(s < chips - 1)
            def _():
                spread(s + 1).wait_recv()
                relay(s + 1).start()

        if square:

            @pl.when(s == 1)
            def _():
                handed(1).wait_recv()
                handed(2).wait_recv()
                relay(3).start()

        return carry

    lax.fori_loop(0, chips, step, 0)
    first = pltpu.make_async_copy(sib.at[0, 0], dx_ref.at[0], dx_sem)
    first.start()
    for k, (left, right) in enumerate(((gate_g, rows_all), (up_g, rows_all), (hid, gb))):
        left = left[...].reshape(-1, n * share)
        grad = dot(left, right[...].reshape(-1, depth), TN)
        for t in range(n):
            dw_ref[t, k] = grad[t * share : (t + 1) * share, :].astype(BF)
    first.wait()
    keep_wp.wait()
    for step in range(n - 1):
        over(step).wait()
    for s in range(chips):
        keep(s).wait()
        relay(s).wait_send()
        if s >= chips - 2:
            swap(s).wait_send()
        if s in direct:
            spread(s).wait_send()
        if s > 0:
            push(s).wait()
    if square:
        hand_on(1).wait_send()
        hand_on(2).wait_send()


def ffn(x, grad_branch, weights, w_packed, n, devices):
    rows, depth = x.shape
    chips = devices // 2
    hidden = weights.shape[1]
    share = hidden // n
    vmem = pl.BlockSpec(memory_space=pltpu.VMEM)
    hbm = pl.BlockSpec(memory_space=pl.ANY)
    return pl.pallas_call(
        functools.partial(ffn_kernel, chips),
        out_shape=(
            jax.ShapeDtypeStruct((chips, rows, depth), BF),
            jax.ShapeDtypeStruct((chips, rows, depth), BF),
            jax.ShapeDtypeStruct((n, 3, share, depth), BF),
            jax.ShapeDtypeStruct((n, *w_packed.shape), BF),
        ),
        in_specs=[vmem, hbm, vmem, hbm],
        out_specs=[hbm, hbm, vmem, hbm],
        scratch_shapes=[
            pltpu.VMEM((chips, 2, rows, depth), BF),
            pltpu.VMEM((chips, 2, rows, depth), BF),
        ]
        + [pltpu.VMEM((chips, 2, rows, hidden), BF)] * 3
        + [
            pltpu.VMEM((2, rows, depth), BF),
            pltpu.VMEM((chips, 2, rows, depth), BF),
            pltpu.VMEM((2, 2, rows, depth), BF),
        ]
        + [pltpu.SemaphoreType.DMA((chips,))] * 8
        + [pltpu.SemaphoreType.DMA((3,))] * 2
        + [pltpu.SemaphoreType.DMA((chips,))] * 2
        + [pltpu.SemaphoreType.DMA]
        + [pltpu.SemaphoreType.DMA((n - 1,))] * 2
        + [pltpu.SemaphoreType.DMA],
        compiler_params=pltpu.CompilerParams(
            vmem_limit_bytes=60 << 20, collective_id=3, has_side_effects=True
        ),
        cost_estimate=pl.CostEstimate(
            flops=2 * 9 * devices * rows * depth * hidden, bytes_accessed=30 << 20, transcendentals=0
        ),
        name="ffn",
    )(x, grad_branch, weights, w_packed)


def unpack_kernel(share, g_ref, gate_ref, up_ref, down_ref, out_ref):
    g = g_ref[0].astype(F32)
    gate_ref[...] = g[:share].T
    up_ref[...] = g[share : 2 * share].T
    down_ref[...] = g[2 * share : 3 * share]
    out_ref[...] = g[3 * share :]


def unpack(grads, share, width):
    devices, height, depth = grads.shape
    hidden = devices * share
    if share % 128:
        gate, up, down = (
            grads[:, k * share : (k + 1) * share].reshape(hidden, depth).astype(F32) for k in range(3)
        )
        return gate.T, up.T, down, grads[:, 3 * share :].reshape(width, depth).astype(F32)
    column = pl.BlockSpec((depth, share), lambda i: (0, i))
    return pl.pallas_call(
        functools.partial(unpack_kernel, share),
        out_shape=(
            jax.ShapeDtypeStruct((depth, hidden), F32),
            jax.ShapeDtypeStruct((depth, hidden), F32),
            jax.ShapeDtypeStruct((hidden, depth), F32),
            jax.ShapeDtypeStruct((width, depth), F32),
        ),
        grid=(devices,),
        in_specs=[pl.BlockSpec((1, height, depth), lambda i: (i, 0, 0))],
        out_specs=[
            column, column, pl.BlockSpec((share, depth), lambda i: (i, 0)),
            pl.BlockSpec((width // devices, depth), lambda i: (i, 0)),
        ],
        compiler_params=pltpu.CompilerParams(vmem_limit_bytes=40 << 20),
        name="unpack",
    )(grads)


def norm_parts(values):
    centre = jnp.mean(values, axis=-1, keepdims=True)
    centred = values - centre
    inverse = lax.rsqrt(jnp.mean(centred * centred, axis=-1, keepdims=True) + EPS)
    return centred * inverse, inverse


def norm_back(upstream, scaled, inverse, gain):
    through = upstream * gain
    inner = (
        through
        - jnp.mean(through, axis=-1, keepdims=True)
        - scaled * jnp.mean(through * scaled, axis=-1, keepdims=True)
    )
    return inverse * inner, jnp.sum(upstream * scaled, axis=0), jnp.sum(upstream, axis=0)


def pack_weights(w_query, w_key, w_value):
    depth, width = w_query.shape
    key, value = (w.reshape(depth, width // HD, 1, HD) for w in (w_key, w_value))
    both = jnp.concatenate([key, value], axis=2).reshape(depth, 2 * width)
    return jnp.concatenate([both, w_query], axis=1)


def on_device(
    tokens, lengths, ln1_gain, ln1_bias, w_query, w_key, w_value, w_out,
    ln2_gain, ln2_bias, w_gate, w_up, down_weight, cotangent,
):
    n = lax.axis_size("tensor")
    local_rows, depth = tokens.shape
    length = local_rows * n
    width = w_query.shape[1]
    row_ids = lax.axis_index("tensor") * local_rows + lax.iota(jnp.int32, local_rows)
    valid = (row_ids < lengths[0])[:, None]

    inputs = tokens.astype(F32)
    grad_out = jnp.where(valid, cotangent.astype(F32), 0.0)
    devices = lax.axis_size("dp")
    place = lax.axis_index("dp")
    share = w_gate.shape[1] // devices

    q, k, v, cosine, sine, attn_rows, grad_branch, weights = begin(
        tokens, cotangent, ln1_gain, ln1_bias, w_query, w_key, w_value, angle_tables(length),
        w_gate, w_up, down_weight, lengths, n, devices,
    )
    attn_rows = attn_rows.reshape(length, depth)
    weights = lax.all_gather(weights, "tensor", axis=1, tiled=True)

    def row_share(w):
        return lax.dynamic_slice_in_dim(w, place * (depth // devices), depth // devices, 0)

    w_packed = pack_weights(row_share(w_query), row_share(w_key), row_share(w_value))
    context, logsum, context_own, _, w_out_all = att_fwd(
        q, k, v,
        lax.dynamic_slice_in_dim(w_out, place * (width // devices), width // devices, 0),
        n, devices,
    )
    w_out_all = w_out_all.reshape(n, width, depth)
    attn_out = sum(dot(context_own[t], w_out_all[t]).astype(BF).astype(F32) for t in range(n))
    middle = inputs + attn_out
    scaled2, inverse2 = norm_parts(middle)
    ffn_in = (scaled2 * ln2_gain + ln2_bias).astype(BF)
    grad_parts, out_parts, ffn_grads, w_packed = ffn(
        ffn_in, grad_branch, weights, w_packed, n, devices
    )
    grad_ffn_in = sum(grad_parts[p].astype(F32) for p in range(devices // 2))
    grad_norm2, gain2_grad, shift2_grad = norm_back(
        grad_ffn_in, scaled2, inverse2, ln2_gain
    )
    grad_middle = grad_out + grad_norm2
    grad_attn = grad_middle.astype(BF)
    ffn_grads = ffn_grads.reshape(n, 3 * share, depth)
    w_packed = lax.all_gather(w_packed, "dp", axis=0)
    w_packed, ffn_grads = lax.optimization_barrier((w_packed, ffn_grads))
    ffn_grads = lax.psum_scatter(ffn_grads, "tensor", scatter_dimension=0, tiled=True)[0]
    packed, packed_own, out_sums, out_piece = att_bwd(
        grad_attn, w_out_all, context_own, out_parts, q, k, v, context, logsum, cosine, sine, n
    )
    ffn_grads, out_piece = lax.optimization_barrier((ffn_grads, out_piece))
    grads = lax.all_gather(jnp.concatenate([ffn_grads, out_piece]), "dp", axis=0)
    gate_grad, up_grad, down_grad, out_grad = unpack(grads, share, width)
    ffn_out = sum(x.astype(F32) for x in (out_parts[0], *out_sums))
    output = jnp.where(valid, middle + ffn_out, 0.0).astype(BF)
    input_grad, query_grad, key_grad, value_grad, sums = finish(
        attn_rows, packed, packed_own, w_packed, tokens, grad_middle, ln1_gain,
        jnp.stack([gain2_grad, shift2_grad]), width, devices,
    )
    gain1_grad, shift1_grad, gain2_grad, shift2_grad = (sums[i] for i in range(4))
    return (
        output, input_grad, gain1_grad, shift1_grad, query_grad, key_grad, value_grad, out_grad,
        gain2_grad, shift2_grad, gate_grad, up_grad, down_grad,
    )


def solution(mesh):
    rows = P(("dp", "tensor"), None)
    columns = P(None, "tensor")
    parts = P("tensor", None)
    return jax.shard_map(
        on_device,
        mesh=mesh,
        in_specs=(
            rows, P("dp"), P(), P(), columns, columns, columns, parts,
            P(), P(), columns, columns, parts, rows,
        ),
        out_specs=(
            rows, rows, P(), P(), columns, columns, columns, parts,
            P(), P(), columns, columns, parts,
        ),
        check_vma=False,
    )
```

profile of v0, /device:TPU:9, one launch (start us, length us, event | category | flops | bytes accessed | tf_op | source)
XLA Modules:
  0.0 579.6 jit_solution(13199549319825844264)
XLA Ops:
  8.3 1.2 copy-done.4
  9.5 1.2 copy-done.6
  10.8 1.0 copy-done.9
  11.8 1.0 copy-done.10
  12.8 1.0 copy-done.11
  13.9 0.7 copy-done.12
  14.6 0.7 copy-done.13
  15.3 71.9 %begin.1 = (bf16[4,2048,128]{2,1,0:T(8,128)(2,1)S(1)}, bf16[4,2048,128]{2,1,0:T(8,128)(2,1)}, bf16[4,2048,128]{2,1,0:T(8,128)(2,1)}, f32[2048,128]{1,0:T(8,128)S...) custom-call(s32[1]{0:T(128)} %copy.41.limit_ref, ...), custom_call_target="tpu_custom_call" | custom-call | flops 32212254720 | bytes 31457280 | tf_op jit(solution)/shard_map/begin/pallas_call | solution.py:300
  87.2 1.3 copy-done.14
  88.5 1.0 copy-done.20
  89.5 1.0 copy-done.21
  90.5 0.8 constant_dynamic-slice_fusion.2
  91.5 0.9 constant_dynamic-slice_fusion
  92.7 0.7 pad_maximum_fusion.1.wp_ref
  93.4 1.6 copy-done.15
  95.0 1.6 copy-done.16
  96.6 1.6 copy-done.17
  98.2 78.2 %att_fwd.1 = (bf16[2048,256]{1,0:T(8,128)(2,1)S(1)}, f32[2048,128]{1,0:T(8,128)S(1)}, bf16[4,512,256]{2,1,0:T(8,128)(2,1)S(1)}, bf16[4,32,1024]{2,1,0:T(8,128)(2,1)}, bf16[4,8,32,1024]{3,2,1,0:T(8,128)(2,1)S(1)}) custom-call(bf16[4,2048,128]{2,1,0:T(8,128)(2,1)S(1)} %copy-done.15, bf16[4,2048,128]{2,1,0:T(8,128)(2,1)S(1)} %copy-done.16, ...), custom_call_target="tpu_custom_call" | custom-call | flops 17179869184 | bytes 5242880 | tf_op jit(solution)/shard_map/att_fwd/pallas_call | solution.py:438
  176.4 1.0 copy-done.19
  177.6 1.1 copy-done.3
  178.7 0.3 copy-done.18
  179.0 0.4 convolution_convert_fusion.1
  179.5 0.4 convolution_convert_fusion.2
  179.9 0.4 convolution_convert_fusion.3
  180.4 0.3 copy-done.7
  180.7 0.8 fusion.23
  181.6 0.3 multiply_reduce_fusion.1
  181.9 0.9 copy-done.22
  182.8 1.4 add_convert_fusion.x_ref
  184.2 100.2 %ffn.1 = (bf16[4,512,1024]{2,1,0:T(8,128)(2,1)}, bf16[4,512,1024]{2,1,0:T(8,128)(2,1)}, bf16[4,3,128,1024]{3,2,1,0:T(8,128)(2,1)}, bf16[4,128,768]{2,1,0:T(8,128)(2,1)}) custom-call(bf16[512,1024]{1,0:T(8,128)(2,1)} %add_convert_fusion.x_ref, bf16[4,2,512,1024]{3,2,1,0:T(8,128)(2,1)} %get-tuple-element.51.gb_ref, ...), custom_call_target="tpu_custom_call" | custom-call | flops 38654705664 | bytes 31457280 | tf_op jit(solution)/shard_map/ffn/pallas_call | solution.py:1082
  284.5 46.6 %all-gather.8.cloned.1.call-done = bf16[32,128,768]{2,1,0:T(8,128)(2,1)} async-done(((bf16[4,128,768]{2,1,0:T(8,128)(2,1)}), bf16[32,128,768]{2,1,0:T(8,128)(2,1)}) %all-gather.8.cloned.1.call-update) | async-done | bytes 6291472 | tf_op jit(solution)/shard_map/all_gather | solution.py:1226
  331.2 3.2 fusion.19
  334.5 1.0 fusion.2
  335.7 2.2 fusion.20
  337.8 152.1 %att_bwd.1 = (bf16[2048,768]{1,0:T(8,128)(2,1)}, bf16[4,512,768]{2,1,0:T(8,128)(2,1)}, bf16[3,512,1024]{2,1,0:T(8,128)(2,1)}, bf16[32,1024]{1,0:T(8,128)(2,1)}) custom-call(bf16[512,1024]{1,0:T(8,128)(2,1)} %get-tuple-element.84.ga_ref, bf16[4,256,1024]{2,1,0:T(8,128)(2,1)} %bitcast.62, bf16[4,512,256]{2,1,0:T(8,128)(2,1)} %copy-done.8, ...), custom_call_target="tpu_custom_call" | custom-call | flops 42949672960 | bytes 10485760 | tf_op jit(solution)/shard_map/att_bwd/pallas_call | solution.py:671
  490.0 2.1 pad_maximum_fusion
  492.2 0.6 pad_maximum_fusion.5.vec_ref
  492.8 3.8 fusion.1
  496.6 60.4 %finish.1 = (f32[512,1024]{1,0:T(8,128)}, f32[1024,256]{1,0:T(8,128)}, f32[1024,256]{1,0:T(8,128)}, f32[1024,256]{1,0:T(8,128)}, f32[8,1024]{1,0:T(8,128)}) custom-call(bf16[2048,1024]{1,0:T(8,128)(2,1)} %bitcast.82, bf16[2048,768]{1,0:T(8,128)(2,1)} %get-tuple-element.61.pk_ref, bf16[4,512,768]{2,1,0:T(8,128)(2,1)} %get-tuple-element.62.own_ref, ...), custom_call_target="tpu_custom_call" | custom-call | flops 6442450944 | bytes 20971520 | tf_op jit(solution)/shard_map/finish/pallas_call | solution.py:865
  557.0 1.5 fusion.22
  558.5 2.9 copy-done.2
  561.4 5.7 unpack.1
  567.2 1.3 copy.42
  568.5 0.6 copy-done.27
  569.1 1.0 copy.43
  570.1 0.6 copy-done.26
  570.7 1.0 copy.44
  571.7 1.0 copy.45
  (69 shorter events, 1.5 us)
Async XLA Ops:
  7.2 85.5 %copy-start = (bf16[256,1024]{1,0:T(8,128)(2,1)S(1)}, bf16[256,1024]{1,0:T(8,128)(2,1)}, u32[]{:S(2)}) copy-start(bf16[256,1024]{1,0:T(8,128)(2,1)} %param.21) | copy-start | bytes 1572868
  7.2 177.0 %all-gather.6.cloned.1.call-start = ((), (), s32[]{:S(2)}) async-start(), calls=%async_computation.1 | async-start | bytes 3932160 | tf_op jit(solution)/shard_map/all_gather | solution.py:1200
  8.3 1.2 copy-start.4
  9.5 1.2 copy-start.6
  10.8 1.0 copy-start.9
  11.8 1.0 copy-start.10
  12.8 1.0 copy-start.11
  13.9 0.7 copy-start.12
  14.6 0.7 copy-start.13
  87.2 1.3 copy-start.14
  88.5 1.0 copy-start.20
  89.5 1.0 copy-start.21
  90.5 240.7 %all-gather.8.cloned.1.call-start = ((), (), s32[]{:S(2)}) async-start(), calls=%async_computation.3 | async-start | bytes 7077888 | tf_op jit(solution)/shard_map/all_gather | solution.py:1226
  93.4 1.6 copy-start.15
  95.0 1.6 copy-start.16
  96.6 1.6 copy-start.17
  176.4 1.0 copy-start.19
  177.3 1.3 copy-start.3
  177.3 1.7 copy-start.18
  177.3 3.0 copy-start.8
  179.4 1.2 copy-start.7
  181.5 1.3 copy-start.22
  181.5 1.3 copy-start.28
  181.5 1.3 copy-start.29
  284.5 205.5 %reduce-scatter.2.cloned.1.call-start = ((), (), s32[]{:S(2)}) async-start(), calls=%async_computation.2 | async-start | bytes 3932160 | tf_op jit(solution)/shard_map/reduce_scatter | solution.py:1228
  331.2 227.3 %all-gather.10.cloned.1.call-start = ((), (), s32[]{:S(2)}) async-start(), calls=%async_computation.4 | async-start | bytes 7667712 | tf_op jit(solution)/shard_map/all_gather | solution.py:1233
  331.2 3.2 copy-start.23
  334.4 1.2 copy-start.5
  558.5 2.9 copy-start.2
  561.4 5.7 copy-start.24
  567.1 2.0 copy-start.27
  569.1 1.6 copy-start.26
  569.1 2.6 copy-start.25
  569.1 3.5 copy-start.1
Sparse Core Ops, SparseCore 0:
  90.6 93.5 all-gather.5
  284.6 46.4 all-gather.7
  333.4 120.6 reduce-scatter.1
  492.3 63.6 all-gather.9
where the time goes:
time: 589 us; the launch traced here: 580 us
  Pallas kernels  469 us (80%)
  waiting for transfers between devices  46.7 us (8%)
  local copies, waits for them, and re-layouts  31.1 us (5%)
  other arithmetic  15.6 us (3%)
  between operations  15.2 us (3%)
    pallas_call x1, Pallas kernels, att_bwd(): pl.pallas_call(functools.partial(att_bwd_kernel, n, bk, chips), out_shape...  152 us
    pallas_call x1, Pallas kernels, ffn(): pl.pallas_call(functools.partial(ffn_kernel, chips), out_shape=(jax.Shape...  100 us
    pallas_call x1, Pallas kernels, att_fwd(): pl.pallas_call(functools.partial(att_fwd_kernel, n, chips), out_shape=(ja...  78.2 us
    pallas_call x1, Pallas kernels, begin(): pl.pallas_call(functools.partial(begin_kernel, n, chips, chunks), out_sha...  71.9 us
    pallas_call x1, Pallas kernels, finish(): pl.pallas_call(functools.partial(finish_kernel, chips, n, width), out_sha...  60.4 us
    all_gather x1, waiting for transfers between devices, on_device(): w_packed = lax.all_gather(w_packed, 'dp', axis=0)  46.6 us
    unnamed x66, local copies, waits for them, and re-layouts  27.5 us
  transfers between devices with their start and end apart: 4, of which 1 were waited for; matrix products, arithmetic and copies ran while one was open for 3% of the time, Pallas kernels for 50%

commit v1 on v0

--- a/solution.py
+++ b/solution.py
@@ -92,12 +92,17 @@
     pl.semaphore_wait(barrier, n + chips - 2 + both_cores)
 
 
-def begin_kernel(
-    n, chips, chunks, limit_ref, tokens_ref, ct_ref, gain_ref, shift_ref, wq_ref, wk_ref, wv_ref,
-    coarse_ref, fine_ref, sign_ref, gate_ref, up_ref, down_ref,
-    q_ref, k_ref, v_ref, cos_ref, sin_ref, rows_ref, gb_all, share_ref, landed, gb, columns, w_sem,
-    right_send, right_recv, left_send, left_recv, gs_send, gs_recv, gr_send, gr_recv, keep_sem, rows_sem,
+def front_kernel(
+    n, chips, chunks, limit_ref, tokens_ref, ct_ref, gain_ref, shift_ref, coarse_ref, fine_ref, sign_ref,
+    wq_ref, wk_ref, wv_ref, gate_ref, up_ref, down_ref, wo_ref,
+    ctx_ref, lse_ref, q_out, k_out, v_out, cos_out, sin_out, rows_ref, gb_all, w_all, out_ref, wo_z, wo_all,
+    landed, gb, columns, own_w, wqkv, q_ref, k_ref, v_ref, cos_ref, sin_ref,
+    right_send, right_recv, left_send, left_recv, gs_send, gs_recv, gr_send, gr_recv, rows_sem,
+    wr_send, wr_recv, wl_send, wl_recv, send_sem, recv_sem, wz_send, wz_recv, ws_send, ws_recv,
+    wx_send, wx_recv, cut_sem, load_sem, save_sem, keep_sem,
 ):
+    i = pl.program_id(0)
+    steps = pl.num_programs(0)
     me = lax.axis_index("tensor")
     place = lax.axis_index("dp")
     core = lax.rem(place, 2)
@@ -106,6 +111,8 @@
     heads = q_ref.shape[0]
     piece = rows // chunks
     limit = limit_ref[0]
+    s = i // heads
+    h = lax.rem(i, heads)
 
     def over(shard, d, c, send, recv, to):
         part = landed.at[shard, pl.ds(c * piece, piece)]
@@ -123,6 +130,22 @@
     def from_right(d, c):
         return over(me + d, d - 1, c, left_send, left_recv, me + 1)
 
+    def weights(shard, d, k, send, recv, to):
+        there = w_all.at[k, shard]
+        return remote(there if d else own_w.at[k], there, send.at[d, k], recv.at[d, k], tensor=to)
+
+    def w_right(d, k):
+        return weights(me - d, d, k, wr_send, wr_recv, me + 1)
+
+    def w_left(d, k):
+        return weights(me + d, d, k, wl_send, wl_recv, me - 1)
+
+    def w_from_left(d, k):
+        return weights(me - d, d - 1, k, wr_send, wr_recv, me - 1)
+
+    def w_from_right(d, k):
+        return weights(me + d, d - 1, k, wl_send, wl_recv, me + 1)
+
     def spread_gb(c):
         return remote(
             gb, gb_all.at[place // 2, core], gs_send.at[c], gs_recv.at[c], dp=same_core(c, chips)
@@ -132,214 +155,6 @@
         there = gb_all.at[differ(place // 2, c, bits), core]
         return remote(there if c else gb, there, gr_send.at[c], gr_recv.at[c], dp=sibling())
 
-    barrier = pltpu.get_barrier_semaphore()
-    pl.semaphore_signal(barrier, inc=1, device_id={"dp": sibling()}, device_id_type=MESH)
-    for s in range(1, chips):
-        to = same_core(s, chips)
-        pl.semaphore_signal(barrier, inc=1, device_id={"dp": to}, device_id_type=MESH)
-
-    @pl.when(me > 0)
-    def _():
-        pl.semaphore_signal(barrier, inc=1, device_id={"tensor": me - 1}, device_id_type=MESH)
-
-    @pl.when(me < n - 1)
-    def _():
-        pl.semaphore_signal(barrier, inc=1, device_id={"tensor": me + 1}, device_id_type=MESH)
-
-    values = tokens_ref[...].astype(F32)
-    values = values - jnp.mean(values, axis=1, keepdims=True)
-    inverse = lax.rsqrt(jnp.mean(values * values, axis=1, keepdims=True) + EPS)
-    landed[me] = (values * inverse * gain_ref[...] + shift_ref[...]).astype(BF)
-
-    pl.semaphore_wait(barrier, chips + jnp.minimum(me, 1) + jnp.minimum(n - 1 - me, 1))
-
-    for c in range(chunks):
-
-        @pl.when(me < n - 1)
-        def _():
-            rightward(0, c).start()
-
-        @pl.when(me > 0)
-        def _():
-            leftward(0, c).start()
-
-    row = me * rows + lax.broadcasted_iota(jnp.int32, (rows, depth), 0)
-    gb[...] = jnp.where(row < limit, ct_ref[...].astype(F32), 0.0).astype(BF)
-    for s in range(1, chips):
-        spread_gb(s).start()
-    relay_gb(0).start()
-    keep = pltpu.make_async_copy(gb, gb_all.at[place // 2, core], keep_sem)
-    keep.start()
-    share = share_ref.shape[1]
-    aligned = share % 128 == 0
-    ours = pl.ds(pl.multiple_of(place * share, share), share)
-    cuts = [pltpu.make_async_copy(down_ref.at[ours], share_ref.at[2], w_sem.at[2])]
-    for k, ref in enumerate((gate_ref, up_ref)):
-        src = ref.at[:, ours] if aligned else ref
-        cuts.append(pltpu.make_async_copy(src, columns.at[k], w_sem.at[k]))
-    for cut in cuts:
-        cut.start()
-
-    lane = lanes((rows, 128))
-    ones = jnp.where(lane < HD + 3, 1.0, 0.0)
-    unit = jnp.where(lane == HD + 3, 1.0, 0.0)
-
-    def put(out_ref, here, values, extra):
-        for h in range(heads):
-            own = values[:, h // 2 * 128 : h // 2 * 128 + 128]
-            own = pltpu.roll(own, HD, 1) if h % 2 else own
-            out_ref[h, here, :] = jnp.where(lane < HD, own, extra).astype(BF)
-
-    def project(shard):
-        here = pl.ds(pl.multiple_of(shard * rows, rows), rows)
-        for i in range(rows // STEP):
-            part = pl.ds(pl.multiple_of(shard * rows + i * STEP, STEP), STEP)
-            coarse = pl.ds(shard * (rows // STEP) + i, 1)
-            c0, s0 = coarse_ref[0, coarse, :], coarse_ref[1, coarse, :]
-            cos_ref[part, :] = c0 * fine_ref[0] - s0 * fine_ref[1]
-            sin_ref[part, :] = (s0 * fine_ref[0] + c0 * fine_ref[1]) * sign_ref[...]
-        cosine = jnp.tile(cos_ref[here, :], (1, heads // 2))
-        sine = jnp.tile(sin_ref[here, :], (1, heads // 2))
-        x = landed[shard]
-        row = shard * rows + lax.broadcasted_iota(jnp.int32, (rows, 128), 0)
-        bias = jnp.where(lane == HD + 3, jnp.where(row < limit, 0.0, -1e30), ones)
-        raw = dot(x, wq_ref[...])
-        turned = (raw * cosine + partner(raw) * sine).astype(BF).astype(F32)
-        put(q_ref, here, turned * SCALE, unit)
-        raw = dot(x, wk_ref[...])
-        put(k_ref, here, raw * cosine + partner(raw) * sine, bias)
-        put(v_ref, here, dot(x, wv_ref[...]), ones)
-
-    def save(shard):
-        return pltpu.make_async_copy(landed.at[shard], rows_ref.at[shard], rows_sem.at[shard])
-
-    for d in range(1, n + 1):
-        for c in range(chunks):
-            if d < n:
-
-                @pl.when(me >= d)
-                def _():
-                    from_left(d, c).wait_recv()
-
-                @pl.when((me >= d) & (me < n - 1))
-                def _():
-                    rightward(d, c).start()
-
-                @pl.when(me + d < n)
-                def _():
-                    from_right(d, c).wait_recv()
-
-                @pl.when((me + d < n) & (me > 0))
-                def _():
-                    leftward(d, c).start()
-
-            if c == 0:
-
-                @pl.when(me >= d - 1)
-                def _():
-                    save(me - d + 1).start()
-                    project(me - d + 1)
-
-            if c == 2 and d == 1:
-                for cut in cuts:
-                    cut.wait()
-                for k in range(2):
-                    share_ref[k] = columns[k].astype(F32).T.astype(BF)
-
-            if c == 1 and d > 1:
-
-                @pl.when(me + d - 1 < n)
-                def _():
-                    save(me + d - 1).start()
-                    project(me + d - 1)
-
-            if c == chunks - 1 and d == 2:
-                for s in range(1, chips // 2 + 1):
-                    spread_gb(s).wait_recv()
-                    relay_gb(s).start()
-
-            if c == 0 and d == n:
-                for s in range(chips // 2 + 1, chips):
-                    spread_gb(s).wait_recv()
-                    relay_gb(s).start()
-
-    for d in range(n - 1):
-        for c in range(chunks):
-
-            @pl.when((me >= d) & (me < n - 1))
-            def _():
-                rightward(d, c).wait_send()
-
-            @pl.when((me + d < n) & (me > 0))
-            def _():
-                leftward(d, c).wait_send()
-
-    for s in range(chips):
-        relay_gb(s).wait()
-        if s:
-            spread_gb(s).wait_send()
-    keep.wait()
-    for shard in range(n):
-        save(shard).wait()
-
-
-def begin(
-    tokens, cotangent, gain, shift, w_query, w_key, w_value, tables, gate, up, down, limit, n, devices
-):
-    rows, depth = tokens.shape
-    total = n * rows
-    heads = w_query.shape[1] // HD
-    chips = devices // 2
-    chunks = 4
-    share = down.shape[0] // devices
-    if share % 128:
-        place = lax.axis_index("dp")
-        gate, up = (lax.dynamic_slice_in_dim(w, place * share, share, 1) for w in (gate, up))
-    vmem = pl.BlockSpec(memory_space=pltpu.VMEM)
-    hbm = pl.BlockSpec(memory_space=pl.ANY)
-    return pl.pallas_call(
-        functools.partial(begin_kernel, n, chips, chunks),
-        out_shape=(jax.ShapeDtypeStruct((heads, total, 128), BF),) * 3
-        + (jax.ShapeDtypeStruct((total, 128), F32),) * 2
-        + (
-            jax.ShapeDtypeStruct((n, rows, depth), BF),
-            jax.ShapeDtypeStruct((chips, 2, rows, depth), BF),
-            jax.ShapeDtypeStruct((3, share, depth), BF),
-        ),
-        in_specs=[pl.BlockSpec(memory_space=pltpu.SMEM)] + [vmem] * 10 + [hbm] * 3,
-        out_specs=[vmem] * 5 + [hbm] * 2 + [vmem],
-        scratch_shapes=[pltpu.VMEM((n, rows, depth), BF), pltpu.VMEM((rows, depth), BF)]
-        + [pltpu.VMEM((2, depth, share), BF), pltpu.SemaphoreType.DMA((3,))]
-        + [pltpu.SemaphoreType.DMA((n - 1, chunks))] * 4
-        + [pltpu.SemaphoreType.DMA((chips,))] * 4
-        + [pltpu.SemaphoreType.DMA, pltpu.SemaphoreType.DMA((n,))],
-        compiler_params=pltpu.CompilerParams(
-            vmem_limit_bytes=44 << 20, collective_id=5, has_side_effects=True
-        ),
-        cost_estimate=pl.CostEstimate(
-            flops=6 * total * depth * heads * HD * 10, bytes_accessed=30 << 20, transcendentals=0
-        ),
-        name="begin",
-    )(
-        limit, tokens, cotangent, gain.reshape(1, depth), shift.reshape(1, depth),
-        w_query, w_key, w_value, *tables, gate, up, down,
-    )
-
-
-def att_fwd_kernel(
-    n, chips, q_ref, k_ref, v_ref, wo_ref,
-    ctx_ref, lse_ref, out_ref, wo_z, wo_all, send_sem, recv_sem, own_sem,
-    wz_send, wz_recv, ws_send, ws_recv, wr_send, wr_recv, keep_sem,
-):
-    s = pl.program_id(0)
-    h = pl.program_id(1)
-    heads = pl.num_programs(1)
-    rows = q_ref.shape[1] // n
-    me = lax.axis_index("tensor")
-    place = lax.axis_index("dp")
-    core = lax.rem(place, 2)
-    bits = chips.bit_length() - 1
-
     def wo_over(step):
         return remote(
             wo_ref, wo_z.at[me], wz_send.at[step], wz_recv.at[step], tensor=ring(n, step + 1)
@@ -352,31 +167,208 @@
 
     def relay_wo(c):
         there = wo_all.at[:, differ(place // 2, c, bits) * 2 + core]
-        return remote(there if c else wo_z, there, wr_send.at[c], wr_recv.at[c], dp=sibling())
-
+        return remote(there if c else wo_z, there, wx_send.at[c], wx_recv.at[c], dp=sibling())
+
+    def push(step):
+        owner = ring(n, step + 1)
+        return remote(
+            ctx_ref.at[pl.ds(pl.multiple_of(owner * rows, rows), rows)], out_ref.at[me],
+            send_sem.at[step], recv_sem.at[step], tensor=owner,
+        )
+
+    def save(shard):
+        return pltpu.make_async_copy(landed.at[shard], rows_ref.at[shard], rows_sem.at[shard])
+
+    mine = pl.ds(pl.multiple_of(me * rows, rows), rows)
     keeps = [
-        pltpu.make_async_copy(wo_ref, wo_z.at[me], keep_sem.at[0]),
-        pltpu.make_async_copy(wo_z, wo_all.at[:, place], keep_sem.at[1]),
+        pltpu.make_async_copy(gb, gb_all.at[place // 2, core], keep_sem.at[0]),
+        pltpu.make_async_copy(wo_ref, wo_z.at[me], keep_sem.at[1]),
+        pltpu.make_async_copy(wo_z, wo_all.at[:, place], keep_sem.at[2]),
+        pltpu.make_async_copy(ctx_ref.at[mine], out_ref.at[me], keep_sem.at[3]),
+        pltpu.make_async_copy(own_w, w_all.at[:, me], keep_sem.at[4]),
     ]
-
-    @pl.when((s == 0) & (h == 0))
-    def _():
-        greet(n, chips, True)
+    saves = [
+        pltpu.make_async_copy(a, b, save_sem.at[j])
+        for j, (a, b) in enumerate(
+            ((q_ref, q_out), (k_ref, k_out), (v_ref, v_out), (cos_ref, cos_out), (sin_ref, sin_out))
+        )
+    ]
+
+    @pl.when(i == 0)
+    def _():
+        loads = [
+            pltpu.make_async_copy(ref, wqkv.at[j], load_sem.at[j])
+            for j, ref in enumerate((wq_ref, wk_ref, wv_ref))
+        ]
+        share = own_w.shape[1]
+        ours = pl.ds(pl.multiple_of(place * share, share), share)
+        cuts = [pltpu.make_async_copy(down_ref.at[ours], own_w.at[2], cut_sem.at[2])]
+        for k, ref in enumerate((gate_ref, up_ref)):
+            src = ref if share % 128 else ref.at[:, ours]
+            cuts.append(pltpu.make_async_copy(src, columns.at[k], cut_sem.at[k]))
+        for copy in loads + cuts:
+            copy.start()
+
+        barrier = pltpu.get_barrier_semaphore()
+        for step in range(1, n):
+            to = ring(n, step)
+            pl.semaphore_signal(barrier, inc=1, device_id={"tensor": to}, device_id_type=MESH)
+        pl.semaphore_signal(barrier, inc=1, device_id={"dp": sibling()}, device_id_type=MESH)
+        for c in range(1, chips):
+            to = same_core(c, chips)
+            pl.semaphore_signal(barrier, inc=1, device_id={"dp": to}, device_id_type=MESH)
+
+        values = tokens_ref[...].astype(F32)
+        values = values - jnp.mean(values, axis=1, keepdims=True)
+        inverse = lax.rsqrt(jnp.mean(values * values, axis=1, keepdims=True) + EPS)
+        landed[me] = (values * inverse * gain_ref[...] + shift_ref[...]).astype(BF)
+
+        pl.semaphore_wait(barrier, n - 1 + chips)
+
+        for c in range(chunks):
+
+            @pl.when(me < n - 1)
+            def _():
+                rightward(0, c).start()
+
+            @pl.when(me > 0)
+            def _():
+                leftward(0, c).start()
+
+        row = me * rows + lax.broadcasted_iota(jnp.int32, (rows, depth), 0)
+        gb[...] = jnp.where(row < limit, ct_ref[...].astype(F32), 0.0).astype(BF)
+        for c in range(1, chips):
+            spread_gb(c).start()
+        relay_gb(0).start()
+        keeps[0].start()
+        keeps[1].start()
+        for copy in loads:
+            copy.wait()
+
+        lane = lanes((rows, 128))
+        ones = jnp.where(lane < HD + 3, 1.0, 0.0)
+        unit = jnp.where(lane == HD + 3, 1.0, 0.0)
+
+        def put(out, here, values, extra):
+            for head in range(heads):
+                own = values[:, head // 2 * 128 : head // 2 * 128 + 128]
+                own = pltpu.roll(own, HD, 1) if head % 2 else own
+                out[head, here, :] = jnp.where(lane < HD, own, extra).astype(BF)
+
+        def project(shard):
+            here = pl.ds(pl.multiple_of(shard * rows, rows), rows)
+            for j in range(rows // STEP):
+                part = pl.ds(pl.multiple_of(shard * rows + j * STEP, STEP), STEP)
+                coarse = pl.ds(shard * (rows // STEP) + j, 1)
+                c0, s0 = coarse_ref[0, coarse, :], coarse_ref[1, coarse, :]
+                cos_ref[part, :] = c0 * fine_ref[0] - s0 * fine_ref[1]
+                sin_ref[part, :] = (s0 * fine_ref[0] + c0 * fine_ref[1]) * sign_ref[...]
+            cosine = jnp.tile(cos_ref[here, :], (1, heads // 2))
+            sine = jnp.tile(sin_ref[here, :], (1, heads // 2))
+            x = landed[shard]
+            row = shard * rows + lax.broadcasted_iota(jnp.int32, (rows, 128), 0)
+            bias = jnp.where(lane == HD + 3, jnp.where(row < limit, 0.0, -1e30), ones)
+            raw = dot(x, wqkv[0])
+            turned = (raw * cosine + partner(raw) * sine).astype(BF).astype(F32)
+            put(q_ref, here, turned * SCALE, unit)
+            raw = dot(x, wqkv[1])
+            put(k_ref, here, raw * cosine + partner(raw) * sine, bias)
+            put(v_ref, here, dot(x, wqkv[2]), ones)
+
+        for d in range(1, n + 1):
+            for c in range(chunks):
+                if d < n:
+
+                    @pl.when(me >= d)
+                    def _():
+                        from_left(d, c).wait_recv()
+
+                    @pl.when((me >= d) & (me < n - 1))
+                    def _():
+                        rightward(d, c).start()
+
+                    @pl.when(me + d < n)
+                    def _():
+                        from_right(d, c).wait_recv()
+
+                    @pl.when((me + d < n) & (me > 0))
+                    def _():
+                        leftward(d, c).start()
+
+                if c == 0:
+
+                    @pl.when(me >= d - 1)
+                    def _():
+                        save(me - d + 1).start()
+                        project(me - d + 1)
+
+                if c == 1 and d > 1:
+
+                    @pl.when(me + d - 1 < n)
+                    def _():
+                        save(me + d - 1).start()
+                        project(me + d - 1)
+
+                if c == 2 and d == 1:
+                    for cut in cuts:
+                        cut.wait()
+                    for k in range(2):
+                        own_w[k] = columns[k].astype(F32).T.astype(BF)
+                    keeps[4].start()
+
+                if c == chunks - 1 and d == 2:
+                    for near in range(1, chips // 2 + 1):
+                        spread_gb(near).wait_recv()
+                        relay_gb(near).start()
+
+            if d < n:
+
+                @pl.when((me < n - 1) & (me + 1 == d))
+                def _():
+                    for k in range(3):
+                        w_right(0, k).start()
+
+                @pl.when((me > 0) & (n - me == d))
+                def _():
+                    for k in range(3):
+                        w_left(0, k).start()
+
+        for copy in saves:
+            copy.start()
         for step in range(n - 1):
             wo_over(step).start()
-        keeps[0].start()
-
-    @pl.when((s == 1) & (h == 0))
+        for far in range(chips // 2 + 1, chips):
+            spread_gb(far).wait_recv()
+            relay_gb(far).start()
+
+    stride = max((heads * n - 2) // max(n - 2, 1), 1)
+    for d in range(1, n - 1):
+
+        @pl.when(i == 1 + (d - 1) * stride)
+        def _():
+            for k in range(3):
+
+                @pl.when((me >= d) & (me < n - 1))
+                def _():
+                    w_from_left(d, k).wait_recv()
+                    w_right(d, k).start()
+
+                @pl.when((me + d < n) & (me > 0))
+                def _():
+                    w_from_right(d, k).wait_recv()
+                    w_left(d, k).start()
+
+    @pl.when(i == heads)
     def _():
         for step in range(n - 1):
             wo_over(step).wait()
-        keeps[0].wait()
+        keeps[1].wait()
         for c in range(1, chips):
             spread_wo(c).start()
         relay_wo(0).start()
-        keeps[1].start()
-
-    @pl.when((s == n - 1) & (h == 0))
+        keeps[2].start()
+
+    @pl.when(i == (n - 1) * heads)
     def _():
         for c in range(1, chips):
             spread_wo(c).wait_recv()
@@ -396,75 +388,137 @@
     ctx_ref[block, pair] = jnp.where((lane >= HD) == (odd == 1), out, ctx_ref[block, pair])
     lse_ref[block, :] = jnp.where(lane == h, peak + jnp.log(total), lse_ref[block, :])
 
-    def push(step):
-        return pltpu.make_async_remote_copy(
-            src_ref=ctx_ref.at[block],
-            dst_ref=out_ref.at[me],
-            send_sem=send_sem.at[step],
-            recv_sem=recv_sem.at[step],
-            device_id={"tensor": owner},
-            device_id_type=MESH,
-        )
-
     @pl.when((h == heads - 1) & (s < n - 1))
     def _():
         push(s).start()
 
-    @pl.when((h == heads - 1) & (s == n - 1))
-    def _():
-        keep = pltpu.make_async_copy(ctx_ref.at[block], out_ref.at[me], own_sem)
-        keep.start()
+    @pl.when(i == steps - 1)
+    def _():
+        keeps[3].start()
+        for d in range(n - 1):
+            for c in range(chunks):
+
+                @pl.when((me >= d) & (me < n - 1))
+                def _():
+                    rightward(d, c).wait_send()
+
+                @pl.when((me + d < n) & (me > 0))
+                def _():
+                    leftward(d, c).wait_send()
+
+            for k in range(3):
+
+                @pl.when((me >= d) & (me < n - 1))
+                def _():
+                    w_right(d, k).wait_send()
+
+                @pl.when((me + d < n) & (me > 0))
+                def _():
+                    w_left(d, k).wait_send()
+
+        for k in range(3):
+            for d in range(1, n):
+
+                @pl.when((me >= d) & ((me == n - 1) | (d == n - 1)))
+                def _():
+                    w_from_left(d, k).wait_recv()
+
+                @pl.when((me + d < n) & ((me == 0) | (d == n - 1)))
+                def _():
+                    w_from_right(d, k).wait_recv()
+
+        for c in range(chips):
+            relay_gb(c).wait()
+            relay_wo(c).wait()
+            if c:
+                spread_gb(c).wait_send()
+                spread_wo(c).wait_send()
+        for shard in range(n):
+            save(shard).wait()
+        for copy in saves:
+            copy.wait()
         for step in range(n - 1):
             push(step).wait()
-        keep.wait()
-        keeps[1].wait()
-        for c in range(chips):
-            relay_wo(c).wait()
-            if c:
-                spread_wo(c).wait_send()
-
-
-def att_fwd(q, k, v, w_out_piece, n, devices):
-    heads, total, _ = q.shape
-    width = heads * HD
-    rows = total // n
-    share, depth = w_out_piece.shape
+        for j in (0, 2, 3, 4):
+            keeps[j].wait()
+
+
+def front(
+    tokens, cotangent, gain, shift, tables, w_query, w_key, w_value, gate, up, down, w_out, limit, n, devices
+):
+    rows, depth = tokens.shape
+    total = n * rows
+    width = w_query.shape[1]
+    heads = width // HD
     chips = devices // 2
+    chunks = 4
+    place = lax.axis_index("dp")
+    share = down.shape[0] // devices
+    part = width // devices
+    if share % 128:
+        gate, up = (lax.dynamic_slice_in_dim(w, place * share, share, 1) for w in (gate, up))
     hbm = pl.BlockSpec(memory_space=pl.ANY)
 
     def whole(*shape):
         return pl.BlockSpec(shape, lambda *_: (0,) * len(shape), pipeline_mode=pl.Buffered(1))
 
+    def dma(*shape):
+        return pltpu.SemaphoreType.DMA(shape)
+
+    head_array = jax.ShapeDtypeStruct((heads, total, 128), BF)
+    table = jax.ShapeDtypeStruct((total, 128), F32)
+    coarse, fine, sign = tables
     return pl.pallas_call(
-        functools.partial(att_fwd_kernel, n, chips),
+        functools.partial(front_kernel, n, chips, chunks),
         out_shape=(
             jax.ShapeDtypeStruct((total, width), BF),
-            jax.ShapeDtypeStruct((total, 128), F32),
+            table,
+            head_array, head_array, head_array, table, table,
+            jax.ShapeDtypeStruct((n, rows, depth), BF),
+            jax.ShapeDtypeStruct((chips, 2, rows, depth), BF),
+            jax.ShapeDtypeStruct((3, n, share, depth), BF),
             jax.ShapeDtypeStruct((n, rows, width), BF),
-            jax.ShapeDtypeStruct((n, share, depth), BF),
-            jax.ShapeDtypeStruct((n, devices, share, depth), BF),
+            jax.ShapeDtypeStruct((n, part, depth), BF),
+            jax.ShapeDtypeStruct((n, devices, part, depth), BF),
         ),
         grid_spec=pltpu.PrefetchScalarGridSpec(
             num_scalar_prefetch=0,
-            grid=(n, heads),
-            in_specs=[whole(heads, total, 128)] * 3 + [hbm],
-            out_specs=[whole(total, width), whole(total, 128)] + [hbm] * 3,
-            scratch_shapes=[pltpu.SemaphoreType.DMA((n - 1,))] * 2
-            + [pltpu.SemaphoreType.DMA]
-            + [pltpu.SemaphoreType.DMA((n - 1,))] * 2
-            + [pltpu.SemaphoreType.DMA((chips,))] * 4
-            + [pltpu.SemaphoreType.DMA((2,))],
+            grid=(n * heads,),
+            in_specs=[pl.BlockSpec(memory_space=pltpu.SMEM)]
+            + [whole(rows, depth)] * 2
+            + [whole(1, depth)] * 2
+            + [whole(*coarse.shape), whole(*fine.shape), whole(*sign.shape)]
+            + [hbm] * 7,
+            out_specs=[whole(total, width), whole(total, 128)] + [hbm] * 11,
+            scratch_shapes=[
+                pltpu.VMEM((n, rows, depth), BF),
+                pltpu.VMEM((rows, depth), BF),
+                pltpu.VMEM((2, depth, share), BF),
+                pltpu.VMEM((3, share, depth), BF),
+                pltpu.VMEM((3, depth, width), BF),
+            ]
+            + [pltpu.VMEM((heads, total, 128), BF)] * 3
+            + [pltpu.VMEM((total, 128), F32)] * 2
+            + [dma(n - 1, chunks)] * 4
+            + [dma(chips)] * 4
+            + [dma(n)]
+            + [dma(n - 1, 3)] * 4
+            + [dma(n - 1)] * 4
+            + [dma(chips)] * 4
+            + [dma(3), dma(3), dma(5), dma(5)],
         ),
         compiler_params=pltpu.CompilerParams(
-            vmem_limit_bytes=40 << 20, collective_id=1, has_side_effects=True
+            vmem_limit_bytes=52 << 20, collective_id=1, has_side_effects=True
         ),
         cost_estimate=pl.CostEstimate(
-            flops=4 * total * total * 256 * heads,
-            bytes_accessed=10 * total * width,
-            transcendentals=total * total * heads,
-        ),
-        name="att_fwd",
-    )(q, k, v, w_out_piece)
+            flops=4 * total * total * 256 * heads * 3, bytes_accessed=40 << 20, transcendentals=0
+        ),
+        name="front",
+    )(
+        limit, tokens, cotangent, gain.reshape(1, depth), shift.reshape(1, depth), coarse, fine, sign,
+        w_query, w_key, w_value, gate, up, down,
+        lax.dynamic_slice_in_dim(w_out, place * part, part, 0),
+    )
 
 
 def att_bwd_kernel(
@@ -1192,22 +1246,19 @@
     place = lax.axis_index("dp")
     share = w_gate.shape[1] // devices
 
-    q, k, v, cosine, sine, attn_rows, grad_branch, weights = begin(
-        tokens, cotangent, ln1_gain, ln1_bias, w_query, w_key, w_value, angle_tables(length),
-        w_gate, w_up, down_weight, lengths, n, devices,
+    (
+        context, logsum, q, k, v, cosine, sine, attn_rows, grad_branch, weights, context_own, _, w_out_all,
+    ) = front(
+        tokens, cotangent, ln1_gain, ln1_bias, angle_tables(length), w_query, w_key, w_value,
+        w_gate, w_up, down_weight, w_out, lengths, n, devices,
     )
     attn_rows = attn_rows.reshape(length, depth)
-    weights = lax.all_gather(weights, "tensor", axis=1, tiled=True)
+    weights = weights.reshape(3, n * share, depth)
 
     def row_share(w):
         return lax.dynamic_slice_in_dim(w, place * (depth // devices), depth // devices, 0)
 
     w_packed = pack_weights(row_share(w_query), row_share(w_key), row_share(w_value))
-    context, logsum, context_own, _, w_out_all = att_fwd(
-        q, k, v,
-        lax.dynamic_slice_in_dim(w_out, place * (width // devices), width // devices, 0),
-        n, devices,
-    )
     w_out_all = w_out_all.reshape(n, width, depth)
     attn_out = sum(dot(context_own[t], w_out_all[t]).astype(BF).astype(F32) for t in range(n))
     middle = inputs + attn_out
@@ -1224,7 +1275,6 @@
     grad_attn = grad_middle.astype(BF)
     ffn_grads = ffn_grads.reshape(n, 3 * share, depth)
     w_packed = lax.all_gather(w_packed, "dp", axis=0)
-    w_packed, ffn_grads = lax.optimization_barrier((w_packed, ffn_grads))
     ffn_grads = lax.psum_scatter(ffn_grads, "tensor", scatter_dimension=0, tiled=True)[0]
     packed, packed_own, out_sums, out_piece = att_bwd(
         grad_attn, w_out_all, context_own, out_parts, q, k, v, context, logsum, cosine, sine, n

time: 589 us -> 524 us (0.89)
  waiting for transfers between devices: 46.7 us -> 0.58 us
  local copies, waits for them, and re-layouts: 31.1 us -> 19 us
  Pallas kernels: 469 us -> 460 us
    all_gather x1, waiting for transfers between devices: 46.6 us -> 0.01 us  [on_device(): w_packed = lax.all_gather(w_packed, 'dp', axis=0)]
    unnamed x66 -> x40, local copies, waits for them, and re-layouts: 27.5 us -> 13.8 us
    pallas_call x2 -> x1, Pallas kernels: 150 us -> 145 us  [front(): pl.pallas_call(functools.partial(front_kernel, n, chips, chunks), out_sha...]
  transfers between devices with their start and end apart: 4 -> 3, of which waited for: 1 -> 0; matrix products, arithmetic and copies ran while one was open for 3% -> 3% of each run, Pallas kernels for 50% -> 41%
where the time goes in v1:
time: 524 us; the launch traced here: 514 us
  Pallas kernels  460 us (88%)
  local copies, waits for them, and re-layouts  19 us (4%)
  between operations  16.9 us (3%)
  other arithmetic  15.7 us (3%)
    pallas_call x1, Pallas kernels, att_bwd(): pl.pallas_call(functools.partial(att_bwd_kernel, n, bk, chips), out_shape...  150 us
    pallas_call x1, Pallas kernels, front(): pl.pallas_call(functools.partial(front_kernel, n, chips, chunks), out_sha...  145 us
    pallas_call x1, Pallas kernels, ffn(): pl.pallas_call(functools.partial(ffn_kernel, chips), out_shape=(jax.Shape...  98.5 us
    pallas_call x1, Pallas kernels, finish(): pl.pallas_call(functools.partial(finish_kernel, chips, n, width), out_sha...  60.3 us
    unnamed x40, local copies, waits for them, and re-layouts  13.8 us
  transfers between devices with their start and end apart: 3, of which 0 were waited for; matrix products, arithmetic and copies ran while one was open for 3% of the time, Pallas kernels for 41%

profile of v1, /device:TPU:9, one launch (start us, length us, event | category | flops | bytes accessed | tf_op | source)
XLA Modules:
  0.0 514.2 jit_solution(13485507251728080370)
XLA Ops:
  8.0 0.0 reduce-scatter.2.cloned.1.call-start
  8.8 0.1 fusion.13
  9.0 0.1 multiply_cosine_fusion
  9.1 0.9 constant_dynamic-slice_fusion.2
  10.0 0.1 copy.35
  10.1 0.9 constant_dynamic-slice_fusion
  11.0 0.1 copy.36
  11.1 0.1 copy.34
  11.3 1.0 copy-done.3
  12.4 1.0 copy-done.4
  13.4 1.0 copy-done.5
  14.4 0.7 copy-done.6
  15.1 0.7 copy-done.7
  15.8 145.5 %front.1 = (bf16[2048,256]{1,0:T(8,128)(2,1)}, f32[2048,128]{1,0:T(8,128)}, bf16[4,2048,128]{2,1,0:T(8,128)(2,1)}, bf16[4,2048,128]{2,1,0:T(8,128)(2,1)}, bf16[4...) custom-call(s32[1]{0:T(128)} %copy.41.limit_ref, ...), custom_call_target="tpu_custom_call" | custom-call | flops 51539607552 | bytes 41943040 | tf_op jit(solution)/shard_map/front/pallas_call | solution.py:471
  161.3 1.8 fusion.21
  163.1 0.0 copy-done.14
  163.1 0.4 convolution_convert_fusion.1
  163.6 0.4 convolution_convert_fusion.2
  164.0 0.4 convolution_convert_fusion.3
  164.5 0.3 copy-done.13
  164.8 0.8 fusion.23
  165.7 0.3 multiply_reduce_fusion.1
  166.0 0.7 pad_maximum_fusion.1.wp_ref
  166.7 1.4 add_convert_fusion.x_ref
  168.1 98.5 %ffn.1 = (bf16[4,512,1024]{2,1,0:T(8,128)(2,1)}, bf16[4,512,1024]{2,1,0:T(8,128)(2,1)}, bf16[4,3,128,1024]{3,2,1,0:T(8,128)(2,1)}, bf16[4,128,768]{2,1,0:T(8,128)(2,1)}) custom-call(bf16[512,1024]{1,0:T(8,128)(2,1)} %add_convert_fusion.x_ref, bf16[4,2,512,1024]{3,2,1,0:T(8,128)(2,1)} %get-tuple-element.46.gb_ref, bf16[3,512,1024]{2,1,0:T(8,128)(2,1)} %bitcast.84, ...), custom_call_target="tpu_custom_call" | custom-call | flops 38654705664 | bytes 31457280 | tf_op jit(solution)/shard_map/ffn/pallas_call | solution.py:1136
  266.6 0.0 reduce-scatter.2.cloned.1.call-update
  266.6 0.0 all-gather.5.cloned.1.call-start
  266.7 0.5 all-gather.5.cloned.1.call-update
  267.2 0.0 all-gather.7.cloned.1.call-start
  267.3 3.0 fusion.19
  270.3 1.0 fusion.2
  271.3 0.2 copy-done.9
  271.5 2.4 fusion.20
  273.9 149.8 %att_bwd.1 = (bf16[2048,768]{1,0:T(8,128)(2,1)}, bf16[4,512,768]{2,1,0:T(8,128)(2,1)}, bf16[3,512,1024]{2,1,0:T(8,128)(2,1)}, bf16[32,1024]{1,0:T(8,128)(2,1)}) custom-call(bf16[512,1024]{1,0:T(8,128)(2,1)} %get-tuple-element.80.ga_ref, bf16[4,256,1024]{2,1,0:T(8,128)(2,1)} %bitcast.67, bf16[4,512,256]{2,1,0:T(8,128)(2,1)} %get-tuple-element.44.cown_ref, ...), custom_call_target="tpu_custom_call" | custom-call | flops 42949672960 | bytes 10485760 | tf_op jit(solution)/shard_map/att_bwd/pallas_call | solution.py:725
  423.7 0.0 reduce-scatter.2.cloned.1.call-done
  423.7 2.1 pad_maximum_fusion
  425.9 0.6 pad_maximum_fusion.5.vec_ref
  426.5 3.8 fusion.1
  430.3 60.3 %finish.1 = (f32[512,1024]{1,0:T(8,128)}, f32[1024,256]{1,0:T(8,128)}, f32[1024,256]{1,0:T(8,128)}, f32[1024,256]{1,0:T(8,128)}, f32[8,1024]{1,0:T(8,128)}) custom-call(bf16[2048,1024]{1,0:T(8,128)(2,1)} %bitcast.83, bf16[2048,768]{1,0:T(8,128)(2,1)} %get-tuple-element.59.pk_ref, bf16[4,512,768]{2,1,0:T(8,128)(2,1)} %get-tuple-element.60.own_ref, ...), custom_call_target="tpu_custom_call" | custom-call | flops 6442450944 | bytes 20971520 | tf_op jit(solution)/shard_map/finish/pallas_call | solution.py:919
  490.6 1.5 fusion.22
  492.1 2.9 copy-done.2
  495.1 5.7 %unpack.1 = (f32[1024,1024]{1,0:T(8,128)}, f32[1024,1024]{1,0:T(8,128)}, f32[1024,1024]{1,0:T(8,128)}, f32[256,1024]{1,0:T(8,128)}) custom-call(bf16[8,416,1024]{2,1,0:T(8,128)(2,1)S(1)} %bitcast.62), custom_call_target="tpu_custom_call" | custom-call | tf_op jit(solution)/shard_map/unpack/pallas_call | solution.py:1189
  500.8 1.3 copy.42
  502.1 0.6 copy-done.12
  502.8 1.0 copy.43
  503.7 0.6 copy-done.11
  504.4 1.0 copy.44
  505.3 1.0 copy.45
  (39 shorter events, 0.2 us)
Async XLA Ops:
  8.0 3.3 copy-start
  8.0 415.7 %reduce-scatter.2.cloned.1.call-start = ((), (), s32[]{:S(2)}) async-start(), calls=%async_computation.1 | async-start | bytes 3932160 | tf_op jit(solution)/shard_map/reduce_scatter | solution.py:1278
  11.3 1.0 copy-start.3
  12.4 1.0 copy-start.4
  13.4 1.0 copy-start.5
  14.4 0.7 copy-start.6
  15.1 0.7 copy-start.7
  161.3 1.9 copy-start.14
  163.6 1.2 copy-start.13
  165.7 1.1 copy-start.15
  165.7 1.1 copy-start.16
  266.6 163.7 %all-gather.5.cloned.1.call-start = ((), (), s32[]{:S(2)}) async-start(), calls=%async_computation.2 | async-start | bytes 7077888 | tf_op jit(solution)/shard_map/all_gather | solution.py:1277
  267.2 224.9 %all-gather.7.cloned.1.call-start = ((), (), s32[]{:S(2)}) async-start(), calls=%async_computation.3 | async-start | bytes 7667712 | tf_op jit(solution)/shard_map/all_gather | solution.py:1283
  270.3 1.2 copy-start.9
  492.1 2.9 copy-start.2
  495.1 5.7 %copy-start.8 = (f32[512,1024]{1,0:T(8,128)S(1)}, f32[512,1024]{1,0:T(8,128)}, u32[]{:S(2)}) copy-start(f32[512,1024]{1,0:T(8,128)} %get-tuple-element.114) | copy-start | bytes 6291460
  500.8 2.0 copy-start.12
  502.8 1.6 copy-start.11
  502.8 2.6 copy-start.10
  502.8 3.5 copy-start.1
Sparse Core Ops, SparseCore 0:
  266.7 115.9 reduce-scatter.1
Sparse Core Ops, SparseCore 1:
  269.0 60.4 all-gather.4
  426.0 63.7 all-gather.6

commit v2 on v1

--- a/solution.py
+++ b/solution.py
@@ -95,7 +95,7 @@
 def front_kernel(
     n, chips, chunks, limit_ref, tokens_ref, ct_ref, gain_ref, shift_ref, coarse_ref, fine_ref, sign_ref,
     wq_ref, wk_ref, wv_ref, gate_ref, up_ref, down_ref, wo_ref,
-    ctx_ref, lse_ref, q_out, k_out, v_out, cos_out, sin_out, rows_ref, gb_all, w_all, out_ref, wo_z, wo_all,
+    ctx_ref, lse_ref, wp_ref, q_out, k_out, v_out, cos_out, sin_out, rows_ref, gb_all, w_all, out_ref, wo_z, wo_all,
     landed, gb, columns, own_w, wqkv, q_ref, k_ref, v_ref, cos_ref, sin_ref,
     right_send, right_recv, left_send, left_recv, gs_send, gs_recv, gr_send, gr_recv, rows_sem,
     wr_send, wr_recv, wl_send, wl_recv, send_sem, recv_sem, wz_send, wz_recv, ws_send, ws_recv,
@@ -244,6 +244,17 @@
         keeps[1].start()
         for copy in loads:
             copy.wait()
+
+        cut = wp_ref.shape[0]
+        here = pl.ds(pl.multiple_of(place * cut, cut), cut)
+        first = lanes((cut, 128)) < HD
+        for p in range(heads // 2):
+            at = slice(p * 128, p * 128 + 128)
+            query, key, value = (wqkv[j, here, at].astype(F32) for j in range(3))
+            even = jnp.where(first, key, pltpu.roll(value, HD, 1))
+            odd = jnp.where(first, pltpu.roll(key, HD, 1), value)
+            for slot, values in ((2 * p, even), (2 * p + 1, odd), (heads + p, query)):
+                wp_ref[:, slot * 128 : slot * 128 + 128] = values.astype(BF)
 
         lane = lanes((rows, 128))
         ones = jnp.where(lane < HD + 3, 1.0, 0.0)
@@ -473,6 +484,7 @@
         out_shape=(
             jax.ShapeDtypeStruct((total, width), BF),
             table,
+            jax.ShapeDtypeStruct((depth // devices, 3 * width), BF),
             head_array, head_array, head_array, table, table,
             jax.ShapeDtypeStruct((n, rows, depth), BF),
             jax.ShapeDtypeStruct((chips, 2, rows, depth), BF),
@@ -489,7 +501,8 @@
             + [whole(1, depth)] * 2
             + [whole(*coarse.shape), whole(*fine.shape), whole(*sign.shape)]
             + [hbm] * 7,
-            out_specs=[whole(total, width), whole(total, 128)] + [hbm] * 11,
+            out_specs=[whole(total, width), whole(total, 128), whole(depth // devices, 3 * width)]
+            + [hbm] * 11,
             scratch_shapes=[
                 pltpu.VMEM((n, rows, depth), BF),
                 pltpu.VMEM((rows, depth), BF),
@@ -508,7 +521,7 @@
             + [dma(3), dma(3), dma(5), dma(5)],
         ),
         compiler_params=pltpu.CompilerParams(
-            vmem_limit_bytes=52 << 20, collective_id=1, has_side_effects=True
+            vmem_limit_bytes=60 << 20, collective_id=1, has_side_effects=True
         ),
         cost_estimate=pl.CostEstimate(
             flops=4 * total * total * 256 * heads * 3, bytes_accessed=40 << 20, transcendentals=0
@@ -950,10 +963,10 @@
 
 
 def ffn_kernel(
-    chips, x_ref, gb_ref, w_ref, wp_ref, dx_ref, out_ref, dw_ref, wp_z,
-    rows_all, gb, hid, gate_g, up_g, own, sib, mate,
+    chips, x_ref, gb_ref, w_ref, wp_ref, dx_ref, out_ref, dw_ref, zs_ref, wp_z,
+    rows_all, gb, hid, gate_g, up_g, own, sib, mate, partial, z_left, z_right,
     ag_send, ag_recv, rl_send, rl_recv, sx_send, sx_recv, rs_send, rs_recv, fw_send, fw_recv,
-    gb_sem, out_sem, dx_sem, wp_send, wp_recv, wp_sem,
+    gb_sem, out_sem, dx_sem, wp_send, wp_recv, wp_sem, zr_send, zr_recv, zl_send, zl_recv,
 ):
     bits = chips.bit_length() - 1
     me = lax.axis_index("dp")
@@ -961,8 +974,7 @@
     chip = me // 2
     other = 1 - core
     rows, depth = x_ref.shape
-    n = dw_ref.shape[0]
-    share = dw_ref.shape[2]
+    n, share, _ = dw_ref.shape
 
     def spread(s):
         to = differ(chip, s, bits) * 2 + core
@@ -1103,11 +1115,81 @@
     lax.fori_loop(0, chips, step, 0)
     first = pltpu.make_async_copy(sib.at[0, 0], dx_ref.at[0], dx_sem)
     first.start()
-    for k, (left, right) in enumerate(((gate_g, rows_all), (up_g, rows_all), (hid, gb))):
+    def zr(t, k, to):
+        return remote(
+            partial.at[t, k], z_left.at[t, k], zr_send.at[t, k], zr_recv.at[t, k], tensor=to
+        )
+
+    def zl(t, k, to):
+        return remote(
+            partial.at[t, k], z_right.at[t, k], zl_send.at[t, k], zl_recv.at[t, k], tensor=to
+        )
+
+    def join(t, k, more):
+        partial[t, k] = (partial[t, k].astype(F32) + more[t, k].astype(F32)).astype(BF)
+
+    def weight_grad(left, right):
         left = left[...].reshape(-1, n * share)
-        grad = dot(left, right[...].reshape(-1, depth), TN)
+        return dot(left, right[...].reshape(-1, depth), TN)
+
+    for k, left in enumerate((gate_g, up_g)):
+        grad = weight_grad(left, rows_all)
         for t in range(n):
-            dw_ref[t, k] = grad[t * share : (t + 1) * share, :].astype(BF)
+            partial[t, k] = grad[t * share : (t + 1) * share, :].astype(BF)
+
+        for j in range(n - 1):
+
+            @pl.when(part == 0)
+            def _():
+                zr(n - 1 - j, k, 1).start()
+
+            @pl.when(part == n - 1)
+            def _():
+                zl(j, k, n - 2).start()
+
+    grad = weight_grad(hid, gb)
+    for t in range(n):
+        dw_ref[t] = grad[t * share : (t + 1) * share, :].astype(BF)
+    for k in range(2):
+        for j in range(n - 1):
+            t = n - 1 - j
+
+            @pl.when((part > 0) & (part < t))
+            def _():
+                zr(t, k, part + 1).wait_recv()
+                join(t, k, z_left)
+                zr(t, k, part + 1).start()
+
+            @pl.when((part < n - 1) & (part > j))
+            def _():
+                zl(j, k, part - 1).wait_recv()
+                join(j, k, z_right)
+                zl(j, k, part - 1).start()
+
+        for t in range(n):
+
+            @pl.when((part == t) & (part > 0))
+            def _():
+                zr(t, k, part - 1).wait_recv()
+                join(t, k, z_left)
+
+            @pl.when((part == t) & (part < n - 1))
+            def _():
+                zl(t, k, part + 1).wait_recv()
+                join(t, k, z_right)
+
+            @pl.when(part == t)
+            def _():
+                zs_ref[k] = partial[t, k]
+
+            @pl.when(part < t)
+            def _():
+                zr(t, k, part + 1).wait_send()
+
+            @pl.when(part > t)
+            def _():
+                zl(t, k, part - 1).wait_send()
+
     first.wait()
     keep_wp.wait()
     for step in range(n - 1):
@@ -1138,11 +1220,12 @@
         out_shape=(
             jax.ShapeDtypeStruct((chips, rows, depth), BF),
             jax.ShapeDtypeStruct((chips, rows, depth), BF),
-            jax.ShapeDtypeStruct((n, 3, share, depth), BF),
+            jax.ShapeDtypeStruct((n, share, depth), BF),
+            jax.ShapeDtypeStruct((2, share, depth), BF),
             jax.ShapeDtypeStruct((n, *w_packed.shape), BF),
         ),
         in_specs=[vmem, hbm, vmem, hbm],
-        out_specs=[hbm, hbm, vmem, hbm],
+        out_specs=[hbm, hbm, vmem, vmem, hbm],
         scratch_shapes=[
             pltpu.VMEM((chips, 2, rows, depth), BF),
             pltpu.VMEM((chips, 2, rows, depth), BF),
@@ -1153,14 +1236,16 @@
             pltpu.VMEM((chips, 2, rows, depth), BF),
             pltpu.VMEM((2, 2, rows, depth), BF),
         ]
+        + [pltpu.VMEM((n, 2, share, depth), BF)] * 3
         + [pltpu.SemaphoreType.DMA((chips,))] * 8
         + [pltpu.SemaphoreType.DMA((3,))] * 2
         + [pltpu.SemaphoreType.DMA((chips,))] * 2
         + [pltpu.SemaphoreType.DMA]
         + [pltpu.SemaphoreType.DMA((n - 1,))] * 2
-        + [pltpu.SemaphoreType.DMA],
+        + [pltpu.SemaphoreType.DMA]
+        + [pltpu.SemaphoreType.DMA((n, 2))] * 4,
         compiler_params=pltpu.CompilerParams(
-            vmem_limit_bytes=60 << 20, collective_id=3, has_side_effects=True
+            vmem_limit_bytes=62 << 20, collective_id=3, has_side_effects=True
         ),
         cost_estimate=pl.CostEstimate(
             flops=2 * 9 * devices * rows * depth * hidden, bytes_accessed=30 << 20, transcendentals=0
@@ -1169,37 +1254,23 @@
     )(x, grad_branch, weights, w_packed)
 
 
-def unpack_kernel(share, g_ref, gate_ref, up_ref, down_ref, out_ref):
-    g = g_ref[0].astype(F32)
-    gate_ref[...] = g[:share].T
-    up_ref[...] = g[share : 2 * share].T
-    down_ref[...] = g[2 * share : 3 * share]
-    out_ref[...] = g[3 * share :]
-
-
-def unpack(grads, share, width):
-    devices, height, depth = grads.shape
+def unpack_kernel(g_ref, gate_ref, up_ref):
+    gate_ref[...] = g_ref[0, 0].astype(F32).T
+    up_ref[...] = g_ref[0, 1].astype(F32).T
+
+
+def unpack(grads):
+    devices, _, share, depth = grads.shape
     hidden = devices * share
     if share % 128:
-        gate, up, down = (
-            grads[:, k * share : (k + 1) * share].reshape(hidden, depth).astype(F32) for k in range(3)
-        )
-        return gate.T, up.T, down, grads[:, 3 * share :].reshape(width, depth).astype(F32)
+        return tuple(grads[:, k].reshape(hidden, depth).astype(F32).T for k in range(2))
     column = pl.BlockSpec((depth, share), lambda i: (0, i))
     return pl.pallas_call(
-        functools.partial(unpack_kernel, share),
-        out_shape=(
-            jax.ShapeDtypeStruct((depth, hidden), F32),
-            jax.ShapeDtypeStruct((depth, hidden), F32),
-            jax.ShapeDtypeStruct((hidden, depth), F32),
-            jax.ShapeDtypeStruct((width, depth), F32),
-        ),
+        unpack_kernel,
+        out_shape=(jax.ShapeDtypeStruct((depth, hidden), F32),) * 2,
         grid=(devices,),
-        in_specs=[pl.BlockSpec((1, height, depth), lambda i: (i, 0, 0))],
-        out_specs=[
-            column, column, pl.BlockSpec((share, depth), lambda i: (i, 0)),
-            pl.BlockSpec((width // devices, depth), lambda i: (i, 0)),
-        ],
+        in_specs=[pl.BlockSpec((1, 2, share, depth), lambda i: (i, 0, 0, 0))],
+        out_specs=[column, column],
         compiler_params=pltpu.CompilerParams(vmem_limit_bytes=40 << 20),
         name="unpack",
     )(grads)
@@ -1220,13 +1291,6 @@
         - scaled * jnp.mean(through * scaled, axis=-1, keepdims=True)
     )
     return inverse * inner, jnp.sum(upstream * scaled, axis=0), jnp.sum(upstream, axis=0)
-
-
-def pack_weights(w_query, w_key, w_value):
-    depth, width = w_query.shape
-    key, value = (w.reshape(depth, width // HD, 1, HD) for w in (w_key, w_value))
-    both = jnp.concatenate([key, value], axis=2).reshape(depth, 2 * width)
-    return jnp.concatenate([both, w_query], axis=1)
 
 
 def on_device(
@@ -1247,7 +1311,8 @@
     share = w_gate.shape[1] // devices
 
     (
-        context, logsum, q, k, v, cosine, sine, attn_rows, grad_branch, weights, context_own, _, w_out_all,
+        context, logsum, w_packed, q, k, v, cosine, sine, attn_rows, grad_branch, weights, context_own, _,
+        w_out_all,
     ) = front(
         tokens, cotangent, ln1_gain, ln1_bias, angle_tables(length), w_query, w_key, w_value,
         w_gate, w_up, down_weight, w_out, lengths, n, devices,
@@ -1255,16 +1320,12 @@
     attn_rows = attn_rows.reshape(length, depth)
     weights = weights.reshape(3, n * share, depth)
 
-    def row_share(w):
-        return lax.dynamic_slice_in_dim(w, place * (depth // devices), depth // devices, 0)
-
-    w_packed = pack_weights(row_share(w_query), row_share(w_key), row_share(w_value))
     w_out_all = w_out_all.reshape(n, width, depth)
     attn_out = sum(dot(context_own[t], w_out_all[t]).astype(BF).astype(F32) for t in range(n))
     middle = inputs + attn_out
     scaled2, inverse2 = norm_parts(middle)
     ffn_in = (scaled2 * ln2_gain + ln2_bias).astype(BF)
-    grad_parts, out_parts, ffn_grads, w_packed = ffn(
+    grad_parts, out_parts, down_grad, pair_grads, w_packed = ffn(
         ffn_in, grad_branch, weights, w_packed, n, devices
     )
     grad_ffn_in = sum(grad_parts[p].astype(F32) for p in range(devices // 2))
@@ -1273,15 +1334,17 @@
     )
     grad_middle = grad_out + grad_norm2
     grad_attn = grad_middle.astype(BF)
-    ffn_grads = ffn_grads.reshape(n, 3 * share, depth)
     w_packed = lax.all_gather(w_packed, "dp", axis=0)
-    ffn_grads = lax.psum_scatter(ffn_grads, "tensor", scatter_dimension=0, tiled=True)[0]
+    pair_grads = lax.all_gather(pair_grads, "dp", axis=0)
+    down_grad = lax.psum_scatter(down_grad, "tensor", scatter_dimension=0, tiled=True)[0]
     packed, packed_own, out_sums, out_piece = att_bwd(
         grad_attn, w_out_all, context_own, out_parts, q, k, v, context, logsum, cosine, sine, n
     )
-    ffn_grads, out_piece = lax.optimization_barrier((ffn_grads, out_piece))
-    grads = lax.all_gather(jnp.concatenate([ffn_grads, out_piece]), "dp", axis=0)
-    gate_grad, up_grad, down_grad, out_grad = unpack(grads, share, width)
+    down_grad, out_piece = lax.optimization_barrier((down_grad, out_piece))
+    grads = lax.all_gather(jnp.concatenate([down_grad, out_piece]), "dp", axis=0)
+    gate_grad, up_grad = unpack(pair_grads)
+    down_grad = grads[:, :share].reshape(devices * share, depth).astype(F32)
+    out_grad = grads[:, share:].reshape(width, depth).astype(F32)
     ffn_out = sum(x.astype(F32) for x in (out_parts[0], *out_sums))
     output = jnp.where(valid, middle + ffn_out, 0.0).astype(BF)
     input_grad, query_grad, key_grad, value_grad, sums = finish(

time: 524 us -> 588 us (1.12)
  waiting for transfers between devices: 0.58 us -> 101 us
  Pallas kernels: 460 us -> 419 us
    all_gather x1 -> x2, waiting for transfers between devices: 0.01 us -> 59.7 us  [the longest x1 32.2 us: on_device(): pair_grads = lax.all_gather(pair_grads, 'dp', axis=0)]
    all_gather x1, waiting for transfers between devices: 0.01 us -> 40.5 us  [on_device(): w_packed = lax.all_gather(w_packed, 'dp', axis=0)]
    pallas_call x1, Pallas kernels: 150 us -> 115 us  [att_bwd(): pl.pallas_call(functools.partial(att_bwd_kernel, n, bk, chips), out_shape...]
    pallas_call x1, Pallas kernels: 60.3 us -> 44 us  [finish(): pl.pallas_call(functools.partial(finish_kernel, chips, n, width), out_sha...]
    pallas_call x1, Pallas kernels: 98.5 us -> 110 us  [ffn(): pl.pallas_call(functools.partial(ffn_kernel, chips), out_shape=(jax.Shape...]
    unnamed x40 -> x30, local copies, waits for them, and re-layouts: 13.8 us -> 11 us
  transfers between devices with their start and end apart: 3 -> 4, of which waited for: 0 -> 3; matrix products, arithmetic and copies ran while one was open for 3% -> 3% of each run, Pallas kernels for 41% -> 21%
where the time goes in v2:
time: 588 us; the launch traced here: 577 us
  Pallas kernels  419 us (71%)
  waiting for transfers between devices  101 us (17%)
  other arithmetic  21.3 us (4%)
  local copies, waits for them, and re-layouts  17.9 us (3%)
  between operations  15.1 us (3%)
    pallas_call x1, Pallas kernels, front(): pl.pallas_call(functools.partial(front_kernel, n, chips, chunks), out_sha...  146 us
    pallas_call x1, Pallas kernels, att_bwd(): pl.pallas_call(functools.partial(att_bwd_kernel, n, bk, chips), out_shape...  115 us
    pallas_call x1, Pallas kernels, ffn(): pl.pallas_call(functools.partial(ffn_kernel, chips), out_shape=(jax.Shape...  110 us
    pallas_call x1, Pallas kernels, finish(): pl.pallas_call(functools.partial(finish_kernel, chips, n, width), out_sha...  44 us
    all_gather x1, waiting for transfers between devices, on_device(): w_packed = lax.all_gather(w_packed, 'dp', axis=0)  40.5 us
    all_gather x1, waiting for transfers between devices, on_device(): pair_grads = lax.all_gather(pair_grads, 'dp', axis=0)  32.2 us
    all_gather x1, waiting for transfers between devices, on_device(): lax.all_gather(jnp.concatenate([down_grad, out_piece]), 'dp', axis=0)  27.5 us
  transfers between devices with their start and end apart: 4, of which 3 were waited for; matrix products, arithmetic and copies ran while one was open for 3% of the time, Pallas kernels for 21%

profile of v2, /device:TPU:9, one launch (start us, length us, event | category | flops | bytes accessed | tf_op | source)
XLA Modules:
  0.0 577.2 jit_solution(2328013906104218692)
XLA Ops:
  7.2 0.0 reduce-scatter.2.cloned.1.call-start
  7.3 0.5 fusion.18
  7.8 0.1 fusion.13
  7.9 0.1 multiply_cosine_fusion
  8.7 0.6 constant_dynamic-slice_fusion.wo_ref
  9.4 0.6 pad_maximum_fusion.1.fine_ref
  10.0 0.6 pad_maximum_fusion.2.coarse_ref
  10.6 145.6 %front.1 = (bf16[2048,256]{1,0:T(8,128)(2,1)}, f32[2048,128]{1,0:T(8,128)}, bf16[128,768]{1,0:T(8,128)(2,1)}, bf16[4,2048,128]{2,1,0:T(8,128)(2,1)}, bf16[4,2048...) custom-call(s32[1]{0:T(128)} %copy.31.limit_ref, ...), custom_call_target="tpu_custom_call" | custom-call | flops 51539607552 | bytes 41943040 | tf_op jit(solution)/shard_map/front/pallas_call | solution.py:482
  156.3 1.8 fusion.21
  158.1 0.4 convolution_convert_fusion.3
  158.6 0.4 convolution_convert_fusion.2
  159.0 0.4 convolution_convert_fusion.1
  159.5 0.3 copy-done.9
  159.8 0.8 fusion.23
  160.7 0.3 multiply_reduce_fusion.1
  161.0 0.3 copy-done.11
  161.3 0.1 copy-done.12
  161.4 1.4 add_convert_fusion.x_ref
  162.8 109.7 %ffn.1 = (bf16[4,512,1024]{2,1,0:T(8,128)(2,1)}, bf16[4,512,1024]{2,1,0:T(8,128)(2,1)}, bf16[4,128,1024]{2,1,0:T(8,128)(2,1)}, bf16[2,128,1024]{2,1,0:T(8,128)(2,1)}, bf16[4,128,768]{2,1,0:T(8,128)(2,1)}) custom-call(bf16[512,1024]{1,0:T(8,128)(2,1)} %add_convert_fusion.x_ref, bf16[4,2,512,1024]{3,2,1,0:T(8,128)(2,1)} %get-tuple-element.46.gb_ref, ...), custom_call_target="tpu_custom_call" | custom-call | flops 38654705664 | bytes 31457280 | tf_op jit(solution)/shard_map/ffn/pallas_call | solution.py:1218
  272.5 0.3 all-gather.9.cloned.1.call-start
  272.8 3.2 fusion.19
  276.0 1.3 copy-done.5
  277.3 1.0 fusion.2
  278.3 3.5 fusion.20
  281.8 114.8 %att_bwd.1 = (bf16[2048,768]{1,0:T(8,128)(2,1)}, bf16[4,512,768]{2,1,0:T(8,128)(2,1)}, bf16[3,512,1024]{2,1,0:T(8,128)(2,1)}, bf16[32,1024]{1,0:T(8,128)(2,1)}) custom-call(bf16[512,1024]{1,0:T(8,128)(2,1)} %get-tuple-element.80.ga_ref, bf16[4,256,1024]{2,1,0:T(8,128)(2,1)} %bitcast.68, bf16[4,512,256]{2,1,0:T(8,128)(2,1)} %get-tuple-element.44.cown_ref, ...), custom_call_target="tpu_custom_call" | custom-call | flops 42949672960 | bytes 10485760 | tf_op jit(solution)/shard_map/att_bwd/pallas_call | solution.py:738
  396.7 1.7 pad_maximum_fusion
  398.5 0.0 all-gather.11.cloned.1.call-start
  398.5 0.7 all-gather.11.cloned.1.call-update
  399.2 0.3 all-gather.7.cloned.1.call-start
  399.5 0.3 all-gather.7.cloned.1.call-update
  399.8 0.6 pad_maximum_fusion.3.vec_ref
  400.4 3.8 fusion.1
  404.2 27.5 %all-gather.9.cloned.1.call-done = bf16[1280,1024]{1,0:T(8,128)(2,1)} async-done(((bf16[160,1024]{1,0:T(8,128)(2,1)}), bf16[1280,1024]{1,0:T(8,128)(2,1)}) %all-gather.9.cloned.1.call-update) | async-done | bytes 2621456 | tf_op jit(solution)/shard_map/all_gather | solution.py:1344
  431.6 1.8 slice.81
  433.4 1.1 slice.80
  434.5 1.1 bitcast_convert_fusion.1
  435.6 2.6 bitcast_convert_fusion
  438.2 32.2 %all-gather.11.cloned.1.call-done = bf16[16,128,1024]{2,1,0:T(8,128)(2,1)} async-done(((bf16[2,128,1024]{2,1,0:T(8,128)(2,1)}), bf16[16,128,1024]{2,1,0:T(8,128)(2,1)}) %all-gather.11.cloned.1.call-update) | async-done | bytes 4194320 | tf_op jit(solution)/shard_map/all_gather | solution.py:1338
  470.5 2.2 copy-done.2
  472.6 4.7 unpack.1
  477.4 40.5 %all-gather.7.cloned.1.call-done = bf16[32,128,768]{2,1,0:T(8,128)(2,1)} async-done(((bf16[4,128,768]{2,1,0:T(8,128)(2,1)}), bf16[32,128,768]{2,1,0:T(8,128)(2,1)}) %all-gather.7.cloned.1.call-update) | async-done | bytes 6291472 | tf_op jit(solution)/shard_map/all_gather | solution.py:1337
  517.9 44.0 %finish.1 = (f32[512,1024]{1,0:T(8,128)}, f32[1024,256]{1,0:T(8,128)}, f32[1024,256]{1,0:T(8,128)}, f32[1024,256]{1,0:T(8,128)}, f32[8,1024]{1,0:T(8,128)}) custom-call(bf16[2048,1024]{1,0:T(8,128)(2,1)} %bitcast.84, bf16[2048,768]{1,0:T(8,128)(2,1)} %get-tuple-element.60.pk_ref, bf16[4,512,768]{2,1,0:T(8,128)(2,1)} %get-tuple-element.61.own_ref, ...), custom_call_target="tpu_custom_call" | custom-call | flops 6442450944 | bytes 20971520 | tf_op jit(solution)/shard_map/finish/pallas_call | solution.py:932
  561.9 1.5 fusion.22
  563.4 3.2 copy.32
  566.6 1.0 copy.33
  567.6 0.6 copy-done.7
  568.2 1.0 copy.34
  569.2 1.0 copy.35
  (29 shorter events, 0.2 us)
Async XLA Ops:
  7.2 1.6 copy-start
  7.2 389.5 %reduce-scatter.2.cloned.1.call-start = ((), (), s32[]{:S(2)}) async-start(), calls=%async_computation.1 | async-start | bytes 1310720 | tf_op jit(solution)/shard_map/reduce_scatter | solution.py:1339
  156.3 1.9 copy-start.10
  158.6 1.2 copy-start.9
  160.6 2.1 copy-start.3
  160.6 0.7 copy-start.11
  160.6 0.7 copy-start.12
  272.5 159.1 %all-gather.9.cloned.1.call-start = ((), (), s32[]{:S(2)}) async-start(), calls=%async_computation.3 | async-start | bytes 2949120 | tf_op jit(solution)/shard_map/all_gather | solution.py:1344
  272.8 4.5 copy-start.4
  276.0 1.3 copy-start.5
  398.5 72.0 %all-gather.11.cloned.1.call-start = ((), (), s32[]{:S(2)}) async-start(), calls=%async_computation.4 | async-start | bytes 4718592 | tf_op jit(solution)/shard_map/all_gather | solution.py:1338
  399.2 118.7 %all-gather.7.cloned.1.call-start = ((), (), s32[]{:S(2)}) async-start(), calls=%async_computation.2 | async-start | bytes 7077888 | tf_op jit(solution)/shard_map/all_gather | solution.py:1337
  470.5 2.2 copy-start.2
  563.4 3.3 copy-start.8
  566.6 1.6 copy-start.7
  566.6 2.6 copy-start.6
  566.6 3.5 copy-start.1
Sparse Core Ops, SparseCore 0:
  272.7 42.0 reduce-scatter.1
  398.6 33.0 all-gather.8
  433.7 36.7 all-gather.10
  472.3 45.5 all-gather.6

commit v3 on v2

--- a/solution.py
+++ b/solution.py
@@ -535,11 +535,11 @@
 
 
 def att_bwd_kernel(
-    n, bk, chips, ga_ref, wo_ref, cown_ref, parts_ref, q_ref, k_ref, v_ref, ctx_ref, lse_ref,
-    cos_ref, sin_ref, pk_ref, own_ref, sums_ref, og_ref, do, gc, dka, dva, dqs,
+    n, bk, chips, ga_ref, wo_ref, cown_ref, parts_ref, pg_ref, q_ref, k_ref, v_ref, ctx_ref, lse_ref,
+    cos_ref, sin_ref, pk_ref, own_ref, sums_ref, og_ref, pg_all, do, gc, dka, dva, dqs,
     og_full, og_own, og_mate, og_sib, og_land, og_piece, og_z,
     send_sem, recv_sem, out_send, out_recv, pk_send, pk_recv, keep_sem,
-    om_send, om_recv, op_send, op_recv, oz_send, oz_recv,
+    om_send, om_recv, op_send, op_recv, oz_send, oz_recv, gs_send, gs_recv, gr_send, gr_recv, pg_sem,
 ):
     i = pl.program_id(0)
     heads, total, _ = k_ref.shape
@@ -591,6 +591,29 @@
 
         lax.fori_loop(0, n - 1, send, 0)
         do[mine, :] = dot(ga_ref[...], wo_ref[me], NT).astype(BF)
+
+    def pg_spread(s):
+        return remote(pg_ref, pg_all.at[place], gs_send.at[s], gs_recv.at[s], dp=same_core(s, chips))
+
+    def pg_relay(s):
+        there = pg_all.at[differ(place // 2, s, bits) * 2 + core]
+        return remote(there if s else pg_ref, there, gr_send.at[s], gr_recv.at[s], dp=sibling())
+
+    def pg_keep():
+        return pltpu.make_async_copy(pg_ref, pg_all.at[place], pg_sem)
+
+    @pl.when(i == 1)
+    def _():
+        for s in range(1, chips):
+            pg_spread(s).start()
+        pg_relay(0).start()
+        pg_keep().start()
+
+    @pl.when(i == heads * n - 2)
+    def _():
+        for s in range(1, chips):
+            pg_spread(s).wait_recv()
+            pg_relay(s).start()
 
     def og_swap():
         return remote(og_mate, og_sib, om_send, om_recv, dp=sibling())
@@ -713,6 +736,11 @@
         for s in range(1, chips):
             push_out(s).wait()
         og_swap().wait_send()
+        pg_keep().wait()
+        for s in range(chips):
+            pg_relay(s).wait()
+            if s:
+                pg_spread(s).wait_send()
         for s in range(1, chips):
             og_push(s).wait_send()
         for step in range(n - 1):
@@ -723,7 +751,9 @@
                 push_pack(slot, step).wait()
 
 
-def att_bwd(grad_attn, w_out, ctx_own, parts, q, k, v, ctx, lse, cosine, sine, n, bk=512):
+def att_bwd(
+    grad_attn, w_out, ctx_own, parts, pair_grads, q, k, v, ctx, lse, cosine, sine, n, bk=512
+):
     heads, total, _ = q.shape
     width = heads * HD
     rows, depth = grad_attn.shape
@@ -742,15 +772,16 @@
             jax.ShapeDtypeStruct((n, rows, slots * 128), BF),
             jax.ShapeDtypeStruct((chips - 1, rows, depth), BF),
             jax.ShapeDtypeStruct((share, depth), BF),
+            jax.ShapeDtypeStruct((2 * chips, *pair_grads.shape), BF),
         ),
         grid_spec=pltpu.PrefetchScalarGridSpec(
             num_scalar_prefetch=0,
             grid=(heads * n,),
-            in_specs=[whole(rows, depth), whole(n, width, depth), whole(n, rows, width), hbm]
+            in_specs=[whole(rows, depth), whole(n, width, depth), whole(n, rows, width), hbm, hbm]
             + [whole(heads, total, 128)] * 3
             + [whole(total, width)]
             + [whole(total, 128)] * 3,
-            out_specs=[whole(total, slots * 128), hbm, hbm, whole(share, depth)],
+            out_specs=[whole(total, slots * 128), hbm, hbm, whole(share, depth), hbm],
             scratch_shapes=[
                 pltpu.VMEM((total, width), BF),
                 pltpu.VMEM((n - 1, rows, width), BF),
@@ -772,10 +803,12 @@
             + [pltpu.SemaphoreType.DMA((slots,))]
             + [pltpu.SemaphoreType.DMA] * 2
             + [pltpu.SemaphoreType.DMA((chips,))] * 2
-            + [pltpu.SemaphoreType.DMA((n - 1,))] * 2,
+            + [pltpu.SemaphoreType.DMA((n - 1,))] * 2
+            + [pltpu.SemaphoreType.DMA((chips,))] * 4
+            + [pltpu.SemaphoreType.DMA],
         ),
         compiler_params=pltpu.CompilerParams(
-            vmem_limit_bytes=56 << 20, collective_id=2, has_side_effects=True
+            vmem_limit_bytes=60 << 20, collective_id=2, has_side_effects=True
         ),
         cost_estimate=pl.CostEstimate(
             flops=10 * total * total * 256 * heads,
@@ -783,7 +816,7 @@
             transcendentals=total * total * heads,
         ),
         name="att_bwd",
-    )(grad_attn, w_out, ctx_own, parts, q, k, v, ctx, lse, cosine, sine)
+    )(grad_attn, w_out, ctx_own, parts, pair_grads, q, k, v, ctx, lse, cosine, sine)
 
 
 def finish_kernel(
@@ -1335,12 +1368,11 @@
     grad_middle = grad_out + grad_norm2
     grad_attn = grad_middle.astype(BF)
     w_packed = lax.all_gather(w_packed, "dp", axis=0)
-    pair_grads = lax.all_gather(pair_grads, "dp", axis=0)
     down_grad = lax.psum_scatter(down_grad, "tensor", scatter_dimension=0, tiled=True)[0]
-    packed, packed_own, out_sums, out_piece = att_bwd(
-        grad_attn, w_out_all, context_own, out_parts, q, k, v, context, logsum, cosine, sine, n
+    packed, packed_own, out_sums, out_piece, pair_grads = att_bwd(
+        grad_attn, w_out_all, context_own, out_parts, pair_grads, q, k, v, context, logsum, cosine, sine, n
     )
-    down_grad, out_piece = lax.optimization_barrier((down_grad, out_piece))
+    down_grad, out_piece, w_packed = lax.optimization_barrier((down_grad, out_piece, w_packed))
     grads = lax.all_gather(jnp.concatenate([down_grad, out_piece]), "dp", axis=0)
     gate_grad, up_grad = unpack(pair_grads)
     down_grad = grads[:, :share].reshape(devices * share, depth).astype(F32)

time: 588 us -> 513 us (0.87)
  waiting for transfers between devices: 101 us -> 0.6 us
  Pallas kernels: 419 us -> 448 us
    all_gather x1, waiting for transfers between devices: 40.5 us -> 0.03 us  [on_device(): w_packed = lax.all_gather(w_packed, 'dp', axis=0)]
    all_gather x1 -> x0, waiting for transfers between devices: 32.2 us -> none  [on_device(): pair_grads = lax.all_gather(pair_grads, 'dp', axis=0)]
    pallas_call x1, Pallas kernels: 115 us -> 145 us  [att_bwd(): pl.pallas_call(functools.partial(att_bwd_kernel, n, bk, chips), out_shape...]
    all_gather x1, waiting for transfers between devices: 27.5 us -> 0.01 us  [on_device(): lax.all_gather(jnp.concatenate([down_grad, out_piece]), 'dp', axis=0)]
  transfers between devices with their start and end apart: 4 -> 3, of which waited for: 3 -> 0; matrix products, arithmetic and copies ran while one was open for 3% -> 2% of each run, Pallas kernels for 21% -> 38%
where the time goes in v3:
time: 513 us; the launch traced here: 503 us
  Pallas kernels  448 us (87%)
  other arithmetic  19.1 us (4%)
  between operations  16.9 us (3%)
  local copies, waits for them, and re-layouts  15.6 us (3%)
    pallas_call x1, Pallas kernels, front(): pl.pallas_call(functools.partial(front_kernel, n, chips, chunks), out_sha...  146 us
    pallas_call x1, Pallas kernels, att_bwd(): pl.pallas_call(functools.partial(att_bwd_kernel, n, bk, chips), out_shape...  145 us
    pallas_call x1, Pallas kernels, ffn(): pl.pallas_call(functools.partial(ffn_kernel, chips), out_shape=(jax.Shape...  110 us
    pallas_call x1, Pallas kernels, finish(): pl.pallas_call(functools.partial(finish_kernel, chips, n, width), out_sha...  43.1 us
  transfers between devices with their start and end apart: 3, of which 0 were waited for; matrix products, arithmetic and copies ran while one was open for 2% of the time, Pallas kernels for 38%

profile of v3, /device:TPU:9, one launch (start us, length us, event | category | flops | bytes accessed | tf_op | source)
XLA Modules:
  0.0 502.7 jit_solution(7536002855991898825)
XLA Ops:
  8.0 0.0 reduce-scatter.2.cloned.1.call-start
  8.1 0.5 fusion.18
  8.6 0.1 fusion.13
  8.8 0.1 multiply_cosine_fusion
  9.6 0.6 constant_dynamic-slice_fusion.wo_ref
  10.2 0.6 pad_maximum_fusion.1.fine_ref
  10.9 0.6 pad_maximum_fusion.2.coarse_ref
  11.5 145.5 %front.1 = (bf16[2048,256]{1,0:T(8,128)(2,1)}, f32[2048,128]{1,0:T(8,128)}, bf16[128,768]{1,0:T(8,128)(2,1)}, bf16[4,2048,128]{2,1,0:T(8,128)(2,1)}, bf16[4,2048...) custom-call(s32[1]{0:T(128)} %copy.31.limit_ref, ...), custom_call_target="tpu_custom_call" | custom-call | flops 51539607552 | bytes 41943040 | tf_op jit(solution)/shard_map/front/pallas_call | solution.py:482
  157.0 1.8 fusion.21
  158.8 0.1 copy-done.12
  158.9 0.4 convolution_convert_fusion.3
  159.3 0.4 convolution_convert_fusion.2
  159.8 0.4 convolution_convert_fusion.1
  160.2 0.3 copy-done.11
  160.6 0.8 fusion.23
  161.4 0.3 multiply_reduce_fusion.1
  161.8 0.3 copy-done.13
  162.1 0.1 copy-done.14
  162.2 1.4 add_convert_fusion.x_ref
  163.5 109.7 %ffn.1 = (bf16[4,512,1024]{2,1,0:T(8,128)(2,1)}, bf16[4,512,1024]{2,1,0:T(8,128)(2,1)}, bf16[4,128,1024]{2,1,0:T(8,128)(2,1)}, bf16[2,128,1024]{2,1,0:T(8,128)(2,1)}, bf16[4,128,768]{2,1,0:T(8,128)(2,1)}) custom-call(bf16[512,1024]{1,0:T(8,128)(2,1)} %add_convert_fusion.x_ref, bf16[4,2,512,1024]{3,2,1,0:T(8,128)(2,1)} %get-tuple-element.48.gb_ref, ...), custom_call_target="tpu_custom_call" | custom-call | flops 38654705664 | bytes 31457280 | tf_op jit(solution)/shard_map/ffn/pallas_call | solution.py:1251
  273.2 0.0 reduce-scatter.2.cloned.1.call-update
  273.2 0.0 all-gather.5.cloned.1.call-start
  273.3 0.5 all-gather.5.cloned.1.call-update
  273.8 0.3 all-gather.7.cloned.1.call-start
  274.1 3.2 fusion.19
  277.3 1.0 fusion.2
  278.3 0.2 copy-done.7
  278.5 2.2 fusion.20
  280.7 144.8 %att_bwd.1 = (bf16[2048,768]{1,0:T(8,128)(2,1)}, bf16[4,512,768]{2,1,0:T(8,128)(2,1)}, bf16[3,512,1024]{2,1,0:T(8,128)(2,1)}, bf16[32,1024]{1,0:T(8,128)(2,1)}, bf16[8,2,128,1024]{3,2,1,0:T(8,128)(2,1)}) custom-call(bf16[512,1024]{1,0:T(8,128)(2,1)} %get-tuple-element.84.ga_ref, bf16[4,256,1024]{2,1,0:T(8,128)(2,1)} %bitcast.66, ...), custom_call_target="tpu_custom_call" | custom-call | flops 42949672960 | bytes 10485760 | tf_op jit(solution)/shard_map/att_bwd/pallas_call | solution.py:768
  425.5 0.0 reduce-scatter.2.cloned.1.call-done
  425.5 0.0 all-gather.5.cloned.1.call-done
  425.6 1.7 pad_maximum_fusion
  427.3 2.2 copy-done.2
  429.5 5.0 unpack.1
  434.5 0.6 pad_maximum_fusion.3.vec_ref
  435.1 2.8 fusion.1
  437.9 43.1 %finish.1 = (f32[512,1024]{1,0:T(8,128)}, f32[1024,256]{1,0:T(8,128)}, f32[1024,256]{1,0:T(8,128)}, f32[1024,256]{1,0:T(8,128)}, f32[8,1024]{1,0:T(8,128)}) custom-call(bf16[2048,1024]{1,0:T(8,128)(2,1)} %bitcast.82, bf16[2048,768]{1,0:T(8,128)(2,1)} %get-tuple-element.63.pk_ref, bf16[4,512,768]{2,1,0:T(8,128)(2,1)} %get-tuple-element.64.own_ref, ...), custom_call_target="tpu_custom_call" | custom-call | flops 6442450944 | bytes 20971520 | tf_op jit(solution)/shard_map/finish/pallas_call | solution.py:965
  481.1 1.6 fusion.22
  482.7 1.8 slice.81
  484.5 1.1 slice.80
  485.6 2.6 bitcast_convert_fusion
  488.2 1.1 bitcast_convert_fusion.1
  489.3 1.3 copy.32
  490.6 0.6 copy-done.10
  491.3 1.0 copy.33
  492.2 0.6 copy-done.9
  492.9 1.0 copy.34
  493.8 1.0 copy.35
  (30 shorter events, 0.1 us)
Async XLA Ops:
  8.0 1.6 copy-start
  8.0 417.5 %reduce-scatter.2.cloned.1.call-start = ((), (), s32[]{:S(2)}) async-start(), calls=%async_computation.1 | async-start | bytes 1310720 | tf_op jit(solution)/shard_map/reduce_scatter | solution.py:1371
  157.0 1.9 copy-start.12
  159.3 1.2 copy-start.11
  161.4 2.1 copy-start.3
  161.4 0.7 copy-start.13
  161.4 0.7 copy-start.14
  273.2 152.3 %all-gather.5.cloned.1.call-start = ((), (), s32[]{:S(2)}) async-start(), calls=%async_computation.2 | async-start | bytes 7077888 | tf_op jit(solution)/shard_map/all_gather | solution.py:1370
  273.8 208.9 %all-gather.7.cloned.1.call-start = ((), (), s32[]{:S(2)}) async-start(), calls=%async_computation.3 | async-start | bytes 2949120 | tf_op jit(solution)/shard_map/all_gather | solution.py:1376
  274.1 3.2 copy-start.4
  277.3 1.2 copy-start.7
  427.3 2.2 copy-start.2
  429.5 5.6 %copy-start.5 = (bf16[3,512,1024]{2,1,0:T(8,128)(2,1)S(1)}, bf16[3,512,1024]{2,1,0:T(8,128)(2,1)}, u32[]{:S(2)}) copy-start(bf16[3,512,1024]{2,1,0:T(8,128)(2,1)} %get-tuple-element.61) | copy-start | bytes 9437188
  485.5 3.7 copy-start.6
  489.3 2.0 copy-start.10
  491.3 1.6 copy-start.9
  491.3 2.6 copy-start.8
  491.3 3.5 copy-start.1
Sparse Core Ops, SparseCore 0:
  273.4 43.1 reduce-scatter.1
Sparse Core Ops, SparseCore 1:
  275.6 71.5 all-gather.4
  427.4 29.2 all-gather.6

commit v4 on v2

--- a/solution.py
+++ b/solution.py
@@ -625,7 +625,7 @@
             if s:
                 og_push(s).start()
 
-    @pl.when(i == heads + 2)
+    @pl.when(i == heads * n - 6)
     def _():
         joined = og_sib[0].astype(F32)
         for s in range(1, chips):
@@ -634,6 +634,9 @@
         og_piece[...] = joined.astype(BF)
         for step in range(n - 1):
             og_over(step).start()
+
+    @pl.when(i == heads + 1)
+    def _():
         for s in range(1, chips):
             push_out(s).start()
 
@@ -723,7 +726,9 @@
                 push_pack(slot, step).wait()
 
 
-def att_bwd(grad_attn, w_out, ctx_own, parts, q, k, v, ctx, lse, cosine, sine, n, bk=512):
+def att_bwd(
+    grad_attn, w_out, ctx_own, parts, q, k, v, ctx, lse, cosine, sine, n, bk=512
+):
     heads, total, _ = q.shape
     width = heads * HD
     rows, depth = grad_attn.shape
@@ -775,7 +780,7 @@
             + [pltpu.SemaphoreType.DMA((n - 1,))] * 2,
         ),
         compiler_params=pltpu.CompilerParams(
-            vmem_limit_bytes=56 << 20, collective_id=2, has_side_effects=True
+            vmem_limit_bytes=60 << 20, collective_id=2, has_side_effects=True
         ),
         cost_estimate=pl.CostEstimate(
             flops=10 * total * total * 256 * heads,
@@ -787,11 +792,11 @@
 
 
 def finish_kernel(
-    chips, n, width, x_ref, pk_ref, own_ref, w_ref, tokens_ref, middle_ref, gain_ref, vec_ref,
-    input_ref, q_ref, k_ref, v_ref, sums_ref,
+    chips, n, width, x_ref, pk_ref, own_ref, w_ref, tokens_ref, middle_ref, gain_ref, vec_ref, pg_ref,
+    input_ref, q_ref, k_ref, v_ref, sums_ref, pg_all,
     full, mate, sib, land, fin, every, vec_z, vec_dp, vec_me,
     sx_send, sx_recv, rs_send, rs_recv, ag_send, ag_recv, rl_send, rl_recv,
-    vz_send, vz_recv, vd_send, vd_recv, own_sem,
+    vz_send, vz_recv, vd_send, vd_recv, own_sem, gs_send, gs_recv, gr_send, gr_recv, pg_sem,
 ):
     bits = chips.bit_length() - 1
     me = lax.axis_index("dp")
@@ -828,6 +833,14 @@
             dp=lax.rem(me + step + 1, 2 * chips),
         )
 
+    def pg_spread(s):
+        return remote(pg_ref, pg_all.at[me], gs_send.at[s], gs_recv.at[s], dp=same_core(s, chips))
+
+    def pg_relay(s):
+        there = pg_all.at[differ(chip, s, bits) * 2 + core]
+        return remote(there if s else pg_ref, there, gr_send.at[s], gr_recv.at[s], dp=sibling())
+
+    pg_keep = pltpu.make_async_copy(pg_ref, pg_all.at[me], pg_sem)
     barrier = pltpu.get_barrier_semaphore()
     for step in range(n - 1):
         pl.semaphore_signal(barrier, inc=1, device_id={"tensor": ring(n, step + 1)}, device_id_type=MESH)
@@ -874,6 +887,10 @@
     for step in range(n - 1):
         vec_over(step).start()
 
+    for s in range(1, chips):
+        pg_spread(s).start()
+    pg_relay(0).start()
+    pg_keep.start()
     for s in range(1, chips):
         push(s).wait_recv()
         total = total + land[s].astype(F32)
@@ -903,6 +920,9 @@
     for t in range(1, 2 * chips):
         vec = vec + vec_dp[t]
     sums_ref[...] = vec
+    for s in range(1, chips):
+        pg_spread(s).wait_recv()
+        pg_relay(s).start()
     for s in range(chips):
         relay(s).wait()
         swap(s).wait_send()
@@ -920,23 +940,32 @@
             q_ref[rows, out] = g[:, (heads + pair) * 128 : (heads + pair + 1) * 128]
             k_ref[rows, out] = jnp.where(first, a, pltpu.roll(b, HD, 1))
             v_ref[rows, out] = jnp.where(first, pltpu.roll(a, HD, 1), b)
-
-
-def finish(rows_all, packed, own, w_all, tokens, middle, gain, vec, width, devices):
+    pg_keep.wait()
+    for s in range(chips):
+        pg_relay(s).wait()
+        if s:
+            pg_spread(s).wait_send()
+
+
+def finish(
+    rows_all, packed, own, w_all, tokens, middle, gain, vec, pair_grads, width, devices
+):
     n, rows, packs = own.shape
     depth = tokens.shape[1]
     chips = devices // 2
     piece = depth // devices
     vmem = pl.BlockSpec(memory_space=pltpu.VMEM)
+    hbm = pl.BlockSpec(memory_space=pl.ANY)
     out = jax.ShapeDtypeStruct((depth, width), F32)
     return pl.pallas_call(
         functools.partial(finish_kernel, chips, n, width),
         out_shape=(
             jax.ShapeDtypeStruct((rows, depth), F32), out, out, out,
             jax.ShapeDtypeStruct((8, depth), F32),
-        ),
-        in_specs=[vmem] * 8,
-        out_specs=[vmem] * 5,
+            jax.ShapeDtypeStruct((devices, *pair_grads.shape), BF),
+        ),
+        in_specs=[vmem] * 8 + [hbm],
+        out_specs=[vmem] * 5 + [hbm],
         scratch_shapes=[
             pltpu.VMEM((depth, packs), F32),
             pltpu.VMEM((chips, piece, packs), BF),
@@ -951,6 +980,8 @@
         + [pltpu.SemaphoreType.DMA((chips,))] * 8
         + [pltpu.SemaphoreType.DMA((n - 1,))] * 2
         + [pltpu.SemaphoreType.DMA((devices - 1,))] * 2
+        + [pltpu.SemaphoreType.DMA]
+        + [pltpu.SemaphoreType.DMA((chips,))] * 4
         + [pltpu.SemaphoreType.DMA],
         compiler_params=pltpu.CompilerParams(
             vmem_limit_bytes=56 << 20, collective_id=4, has_side_effects=True
@@ -959,7 +990,7 @@
             flops=4 * n * rows * depth * packs, bytes_accessed=20 << 20, transcendentals=0
         ),
         name="finish",
-    )(rows_all, packed, own, w_all, tokens, middle, gain.reshape(1, depth), vec)
+    )(rows_all, packed, own, w_all, tokens, middle, gain.reshape(1, depth), vec, pair_grads)
 
 
 def ffn_kernel(
@@ -1254,26 +1285,43 @@
     )(x, grad_branch, weights, w_packed)
 
 
-def unpack_kernel(g_ref, gate_ref, up_ref):
-    gate_ref[...] = g_ref[0, 0].astype(F32).T
-    up_ref[...] = g_ref[0, 1].astype(F32).T
-
-
-def unpack(grads):
-    devices, _, share, depth = grads.shape
+def unpack_kernel(share, pair_ref, rest_ref, gate_ref, up_ref, down_ref, out_ref):
+    gate_ref[...] = pair_ref[0, 0].astype(F32).T
+    up_ref[...] = pair_ref[0, 1].astype(F32).T
+    rest = rest_ref[0].astype(F32)
+    down_ref[...] = rest[:share]
+    out_ref[...] = rest[share:]
+
+
+def unpack(pair, rest):
+    devices, _, share, depth = pair.shape
     hidden = devices * share
+    height = rest.shape[1]
+    width = devices * (height - share)
     if share % 128:
-        return tuple(grads[:, k].reshape(hidden, depth).astype(F32).T for k in range(2))
+        down = rest[:, :share].reshape(hidden, depth).astype(F32)
+        gate, up = (pair[:, k].reshape(hidden, depth).astype(F32).T for k in range(2))
+        return gate, up, down, rest[:, share:].reshape(width, depth).astype(F32)
     column = pl.BlockSpec((depth, share), lambda i: (0, i))
     return pl.pallas_call(
-        unpack_kernel,
-        out_shape=(jax.ShapeDtypeStruct((depth, hidden), F32),) * 2,
+        functools.partial(unpack_kernel, share),
+        out_shape=(jax.ShapeDtypeStruct((depth, hidden), F32),) * 2
+        + (
+            jax.ShapeDtypeStruct((hidden, depth), F32),
+            jax.ShapeDtypeStruct((width, depth), F32),
+        ),
         grid=(devices,),
-        in_specs=[pl.BlockSpec((1, 2, share, depth), lambda i: (i, 0, 0, 0))],
-        out_specs=[column, column],
+        in_specs=[
+            pl.BlockSpec((1, 2, share, depth), lambda i: (i, 0, 0, 0)),
+            pl.BlockSpec((1, height, depth), lambda i: (i, 0, 0)),
+        ],
+        out_specs=[
+            column, column, pl.BlockSpec((share, depth), lambda i: (i, 0)),
+            pl.BlockSpec((height - share, depth), lambda i: (i, 0)),
+        ],
         compiler_params=pltpu.CompilerParams(vmem_limit_bytes=40 << 20),
         name="unpack",
-    )(grads)
+    )(pair, rest)
 
 
 def norm_parts(values):
@@ -1335,22 +1383,19 @@
     grad_middle = grad_out + grad_norm2
     grad_attn = grad_middle.astype(BF)
     w_packed = lax.all_gather(w_packed, "dp", axis=0)
-    pair_grads = lax.all_gather(pair_grads, "dp", axis=0)
     down_grad = lax.psum_scatter(down_grad, "tensor", scatter_dimension=0, tiled=True)[0]
     packed, packed_own, out_sums, out_piece = att_bwd(
         grad_attn, w_out_all, context_own, out_parts, q, k, v, context, logsum, cosine, sine, n
     )
-    down_grad, out_piece = lax.optimization_barrier((down_grad, out_piece))
+    down_grad, out_piece, w_packed = lax.optimization_barrier((down_grad, out_piece, w_packed))
     grads = lax.all_gather(jnp.concatenate([down_grad, out_piece]), "dp", axis=0)
-    gate_grad, up_grad = unpack(pair_grads)
-    down_grad = grads[:, :share].reshape(devices * share, depth).astype(F32)
-    out_grad = grads[:, share:].reshape(width, depth).astype(F32)
     ffn_out = sum(x.astype(F32) for x in (out_parts[0], *out_sums))
     output = jnp.where(valid, middle + ffn_out, 0.0).astype(BF)
-    input_grad, query_grad, key_grad, value_grad, sums = finish(
+    input_grad, query_grad, key_grad, value_grad, sums, pair_grads = finish(
         attn_rows, packed, packed_own, w_packed, tokens, grad_middle, ln1_gain,
-        jnp.stack([gain2_grad, shift2_grad]), width, devices,
+        jnp.stack([gain2_grad, shift2_grad]), pair_grads, width, devices,
     )
+    gate_grad, up_grad, down_grad, out_grad = unpack(pair_grads, grads)
     gain1_grad, shift1_grad, gain2_grad, shift2_grad = (sums[i] for i in range(4))
     return (
         output, input_grad, gain1_grad, shift1_grad, query_grad, key_grad, value_grad, out_grad,

time: 588 us -> 519 us (0.88)
  the two profiles are of different devices: /device:TPU:9 before, /device:TPU:0 now
where the time goes in v4:
time: 519 us; the launch traced here: 510 us
  Pallas kernels  459 us (88%)
  between operations  16.8 us (3%)
  other arithmetic  16.3 us (3%)
  local copies, waits for them, and re-layouts  14.4 us (3%)
    pallas_call x1, Pallas kernels, front(): pl.pallas_call(functools.partial(front_kernel, n, chips, chunks), out_sha...  150 us
    pallas_call x1, Pallas kernels, att_bwd(): pl.pallas_call(functools.partial(att_bwd_kernel, n, bk, chips), out_shape...  118 us
    pallas_call x1, Pallas kernels, ffn(): pl.pallas_call(functools.partial(ffn_kernel, chips), out_shape=(jax.Shape...  111 us
    pallas_call x1, Pallas kernels, finish(): pl.pallas_call(functools.partial(finish_kernel, chips, n, width), out_sha...  73.6 us
    unnamed x34, local copies, waits for them, and re-layouts  10.4 us
  transfers between devices with their start and end apart: 3, of which 0 were waited for; matrix products, arithmetic and copies ran while one was open for 2% of the time, Pallas kernels for 38%

profile of v4, /device:TPU:0, one launch (start us, length us, event | category | flops | bytes accessed | tf_op | source)
XLA Modules:
  0.0 509.5 jit_solution(2170735043273311837)
XLA Ops:
  8.0 0.0 copy-start
  8.0 0.0 reduce-scatter.2.cloned.1.call-start
  8.1 0.5 fusion.18
  8.6 0.1 fusion.13
  8.8 0.1 multiply_cosine_fusion
  9.6 0.6 constant_dynamic-slice_fusion.wo_ref
  10.2 0.6 pad_maximum_fusion.1.fine_ref
  10.9 0.6 pad_maximum_fusion.2.coarse_ref
  11.5 149.9 %front.1 = (bf16[2048,256]{1,0:T(8,128)(2,1)}, f32[2048,128]{1,0:T(8,128)}, bf16[128,768]{1,0:T(8,128)(2,1)}, bf16[4,2048,128]{2,1,0:T(8,128)(2,1)}, bf16[4,2048...) custom-call(s32[1]{0:T(128)} %copy.31.limit_ref, ...), custom_call_target="tpu_custom_call" | custom-call | flops 51539607552 | bytes 41943040 | tf_op jit(solution)/shard_map/front/pallas_call | solution.py:482
  161.4 1.8 fusion.21
  163.2 0.0 copy-done.12
  163.2 0.4 convolution_convert_fusion.3
  163.7 0.0 copy-start.11
  163.7 0.4 convolution_convert_fusion.2
  164.1 0.4 convolution_convert_fusion.1
  164.6 0.3 copy-done.11
  164.9 0.8 fusion.23
  165.8 0.3 multiply_reduce_fusion.1
  166.2 0.3 copy-done.13
  166.5 0.1 copy-done.14
  166.5 1.4 add_convert_fusion.x_ref
  167.9 111.3 %ffn.1 = (bf16[4,512,1024]{2,1,0:T(8,128)(2,1)}, bf16[4,512,1024]{2,1,0:T(8,128)(2,1)}, bf16[4,128,1024]{2,1,0:T(8,128)(2,1)}, bf16[2,128,1024]{2,1,0:T(8,128)(2,1)}, bf16[4,128,768]{2,1,0:T(8,128)(2,1)}) custom-call(bf16[512,1024]{1,0:T(8,128)(2,1)} %add_convert_fusion.x_ref, bf16[4,2,512,1024]{3,2,1,0:T(8,128)(2,1)} %get-tuple-element.50.gb_ref, ...), custom_call_target="tpu_custom_call" | custom-call | flops 38654705664 | bytes 31457280 | tf_op jit(solution)/shard_map/ffn/pallas_call | solution.py:1249
  279.2 0.0 reduce-scatter.2.cloned.1.call-update
  279.2 0.0 all-gather.5.cloned.1.call-start
  279.3 0.5 all-gather.5.cloned.1.call-update
  279.8 0.3 all-gather.7.cloned.1.call-start
  280.1 3.2 fusion.19
  283.3 1.0 fusion.2
  284.3 0.2 copy-done.7
  284.6 2.2 fusion.20
  286.7 118.3 %att_bwd.1 = (bf16[2048,768]{1,0:T(8,128)(2,1)}, bf16[4,512,768]{2,1,0:T(8,128)(2,1)}, bf16[3,512,1024]{2,1,0:T(8,128)(2,1)}, bf16[32,1024]{1,0:T(8,128)(2,1)}) custom-call(bf16[512,1024]{1,0:T(8,128)(2,1)} %get-tuple-element.88.ga_ref, bf16[4,256,1024]{2,1,0:T(8,128)(2,1)} %bitcast.59, bf16[4,512,256]{2,1,0:T(8,128)(2,1)} %get-tuple-element.48.cown_ref, ...), custom_call_target="tpu_custom_call" | custom-call | flops 42949672960 | bytes 10485760 | tf_op jit(solution)/shard_map/att_bwd/pallas_call | solution.py:743
  405.0 0.0 reduce-scatter.2.cloned.1.call-done
  405.1 0.0 all-gather.5.cloned.1.call-done
  405.1 1.7 pad_maximum_fusion
  406.8 0.0 all-gather.7.cloned.1.call-update
  406.9 0.6 pad_maximum_fusion.3.vec_ref
  407.5 3.8 fusion.1
  411.3 73.6 %finish.1 = (f32[512,1024]{1,0:T(8,128)}, f32[1024,256]{1,0:T(8,128)}, f32[1024,256]{1,0:T(8,128)}, f32[1024,256]{1,0:T(8,128)}, f32[8,1024]{1,0:T(8,128)}, /*index=5*/bf16[8,2,128,1024]{3,2,1,0:T(8,128)(2,1)}) custom-call(bf16[2048,1024]{1,0:T(8,128)(2,1)} %bitcast.75, bf16[2048,768]{1,0:T(8,128)(2,1)} %get-tuple-element.64.pk_ref, ...), custom_call_target="tpu_custom_call" | custom-call | flops 6442450944 | bytes 20971520 | tf_op jit(solution)/shard_map/finish/pallas_call | solution.py:960
  484.9 1.5 fusion.22
  486.5 2.2 copy-done.2
  488.6 1.7 copy-done.3
  490.4 5.7 %unpack.1 = (f32[1024,1024]{1,0:T(8,128)}, f32[1024,1024]{1,0:T(8,128)}, f32[1024,1024]{1,0:T(8,128)}, f32[256,1024]{1,0:T(8,128)}) custom-call(bf16[8,2,128,1024]{3,2,1,0:T(8,128)(2,1)S(1)} %copy-done.2, bf16[8,160,1024]{2,1,0:T(8,128)(2,1)S(1)} %bitcast.58), custom_call_target="tpu_custom_call" | custom-call | tf_op jit(solution)/shard_map/unpack/pallas_call | solution.py:1306
  496.1 1.3 copy.32
  497.5 0.6 copy-done.10
  498.1 1.0 copy.33
  499.1 0.6 copy-done.9
  499.7 1.0 copy.34
  500.7 1.0 copy.35
  (26 shorter events, 0.1 us)
Async XLA Ops:
  8.0 1.6 copy-start
  8.0 397.0 %reduce-scatter.2.cloned.1.call-start = ((), (), s32[]{:S(2)}) async-start(), calls=%async_computation.1 | async-start | bytes 1310720 | tf_op jit(solution)/shard_map/reduce_scatter | solution.py:1386
  161.4 1.9 copy-start.12
  163.7 1.2 copy-start.11
  165.8 2.1 copy-start.4
  165.8 0.7 copy-start.13
  165.8 0.7 copy-start.14
  279.2 125.9 %all-gather.5.cloned.1.call-start = ((), (), s32[]{:S(2)}) async-start(), calls=%async_computation.2 | async-start | bytes 7077888 | tf_op jit(solution)/shard_map/all_gather | solution.py:1385
  279.8 206.6 %all-gather.7.cloned.1.call-start = ((), (), s32[]{:S(2)}) async-start(), calls=%async_computation.3 | async-start | bytes 2949120 | tf_op jit(solution)/shard_map/all_gather | solution.py:1391
  280.1 3.2 copy-start.5
  283.3 1.2 copy-start.7
  486.5 2.2 copy-start.2
  488.6 1.7 copy-start.3
  490.4 5.7 %copy-start.6 = (f32[512,1024]{1,0:T(8,128)S(1)}, f32[512,1024]{1,0:T(8,128)}, u32[]{:S(2)}) copy-start(f32[512,1024]{1,0:T(8,128)} %get-tuple-element.122) | copy-start | bytes 6291460
  496.1 2.0 copy-start.10
  498.1 1.6 copy-start.9
  498.1 2.6 copy-start.8
  498.1 3.5 copy-start.1
Sparse Core Ops, SparseCore 0:
  279.4 34.8 reduce-scatter.1
Sparse Core Ops, SparseCore 1:
  281.6 65.6 all-gather.4
  406.9 43.4 all-gather.6
